TPU v7x, 8 devices: a whole 2x2x1 slice. The times are simulated.
8 devices in a mesh: rep: 2 (over z, y), grp: 4 (over x, core).
Axes of the slice: x: 2, y: 2, z: 1, core: 2. Of those that a mesh axis runs over, the one named last changes fastest.
Arguments:
- x_in: bfloat16 [512, 2048], P(('rep', 'grp')), parts along dimension 0
- seq_len: int32 [512], P(('rep', 'grp')), parts along dimension 0
- k_cache: bfloat16 [512, 256, 2, 128], P(('rep', 'grp')), parts along dimension 0
- v_cache: bfloat16 [512, 256, 2, 128], P(('rep', 'grp')), parts along dimension 0
- gamma_attn: bfloat16 [2048], replicated
- w_qkv: bfloat16 [2048, 2560], replicated
- b_qkv: bfloat16 [2560], replicated
- w_proj: bfloat16 [2048, 2048], replicated
- gamma_mlp: bfloat16 [2048], replicated
- w_in: bfloat16 [2, 11008, 2048], P(None, 'grp')
- w_out: bfloat16 [11008, 2048], P('grp')
Outputs:
- output 1: bfloat16 [512, 2048], P(('rep', 'grp')), parts along dimension 0
- output 2: bfloat16 [512, 256, 2, 128], P(('rep', 'grp')), parts along dimension 0
- output 3: bfloat16 [512, 256, 2, 128], P(('rep', 'grp')), parts along dimension 0
There are 2 independent parts. A program takes and returns all parts, laid end to end along the dimension named above; an argument that names none is the same for every part.
All inputs are finite; a program needn't handle non-finite values.
Results may differ from a plain program's by a relative error of at most 0.00743079.
Values are sent between devices in bfloat16 or wider.
A program may use at most 1 GiB of HBM per device.

v0:
```python
import jax
import jax.numpy as jnp
from jax import lax
from jax.sharding import PartitionSpec as P

HEAD_DIM = 128
ROPE_BASE = 10000.0
EPS = 1e-5


def rms_norm(vals, gain):
    mean_sq = jnp.mean(vals * vals, axis=-1, keepdims=True)
    return (vals * lax.rsqrt(mean_sq + EPS) * gain.astype(jnp.float32)).astype(jnp.bfloat16)


def rotary(vals, positions):
    rot_dim = HEAD_DIM // 2
    inv_freq = ROPE_BASE ** (-jnp.arange(0, rot_dim, 2, dtype=jnp.float32) / rot_dim)
    angles = positions.astype(jnp.float32)[:, None] * inv_freq[None, :]
    cosine = jnp.cos(angles)[:, None, :]
    sine = jnp.sin(angles)[:, None, :]
    pairs = vals[..., :rot_dim].reshape(vals.shape[:-1] + (rot_dim // 2, 2))
    even_part = pairs[..., 0]
    odd_part = pairs[..., 1]
    rotated = jnp.stack([even_part * cosine - odd_part * sine, odd_part * cosine + even_part * sine], axis=-1)
    return jnp.concatenate([rotated.reshape(vals.shape[:-1] + (rot_dim,)), vals[..., rot_dim:]], axis=-1)


def attention_block(x_in, seq_len, k_cache, v_cache, gamma_attn, w_qkv, b_qkv, w_proj):
    batch_rows, cache_len, kv_heads = k_cache.shape[0], k_cache.shape[1], k_cache.shape[2]
    num_heads = w_proj.shape[0] // HEAD_DIM
    q_width = num_heads * HEAD_DIM
    kv_width = kv_heads * HEAD_DIM
    x_f32 = x_in.astype(jnp.float32)
    normed = rms_norm(x_f32, gamma_attn)
    qkv_proj = jnp.dot(normed, w_qkv, preferred_element_type=jnp.float32) + b_qkv.astype(jnp.float32)
    query_rot = rotary(qkv_proj[:, :q_width].reshape(batch_rows, num_heads, HEAD_DIM), seq_len).astype(jnp.bfloat16)
    key_new = rotary(qkv_proj[:, q_width:q_width + kv_width].reshape(batch_rows, kv_heads, HEAD_DIM), seq_len).astype(jnp.bfloat16)
    value_new = qkv_proj[:, q_width + kv_width:].reshape(batch_rows, kv_heads, HEAD_DIM).astype(jnp.bfloat16)
    positions = jnp.arange(cache_len, dtype=jnp.int32)
    at_len = (positions[None, :] == seq_len[:, None])[:, :, None, None]
    k_out = jnp.where(at_len, key_new[:, None], k_cache)
    v_out = jnp.where(at_len, value_new[:, None], v_cache)
    q_grouped = query_rot.reshape(batch_rows, kv_heads, num_heads // kv_heads, HEAD_DIM)
    attn_scores = jnp.einsum('bgqd,blgd->bgql', q_grouped, k_out, preferred_element_type=jnp.float32) * HEAD_DIM ** -0.5
    visible = (positions[None, :] <= seq_len[:, None])[:, None, None, :]
    attn_probs = jax.nn.softmax(jnp.where(visible, attn_scores, -jnp.inf), axis=-1).astype(jnp.bfloat16)
    context = jnp.einsum('bgql,blgd->bgqd', attn_probs, v_out, preferred_element_type=jnp.float32)
    context = context.astype(jnp.bfloat16).reshape(batch_rows, q_width)
    hidden = x_f32 + jnp.dot(context, w_proj, preferred_element_type=jnp.float32)
    return hidden, k_out, v_out


def solution(mesh):
    row_spec = P(('rep', 'grp'))
    repl_spec = P()

    def local_layer(x_in, seq_len, k_cache, v_cache, gamma_attn, w_qkv, b_qkv, w_proj, gamma_mlp, w_in, w_out):
        hidden, k_out, v_out = attention_block(x_in, seq_len, k_cache, v_cache, gamma_attn, w_qkv, b_qkv, w_proj)
        mlp_in = rms_norm(hidden, gamma_mlp)
        group_rows = lax.all_gather(mlp_in, 'grp', axis=0, tiled=True)
        gate_up = jnp.einsum('bh,cfh->bcf', group_rows, w_in, preferred_element_type=jnp.float32)
        swiglu = (jax.nn.silu(gate_up[:, 0]) * gate_up[:, 1]).astype(jnp.bfloat16)
        part_sum = jnp.dot(swiglu, w_out, preferred_element_type=jnp.float32).astype(jnp.bfloat16)
        mlp_out = lax.psum_scatter(part_sum, 'grp', scatter_dimension=0, tiled=True)
        layer_out = (hidden + mlp_out.astype(jnp.float32)).astype(jnp.bfloat16)
        return layer_out, k_out, v_out

    return jax.shard_map(local_layer, mesh=mesh,
                         in_specs=(row_spec, row_spec, row_spec, row_spec, repl_spec, repl_spec, repl_spec,
                                   repl_spec, repl_spec, P(None, 'grp', None), P('grp', None)),
                         out_specs=(row_spec, row_spec, row_spec), check_vma=False)
```

profile of v0, /device:TPU:0, one launch (start us, length us, event | category | flops | bytes accessed | tf_op | source)
XLA Modules:
  0.0 125.9 jit_solution(5724808038460555990)
XLA Ops:
  7.2 0.7 convert_element_type.59
  7.9 0.7 iota_compare_fusion.1
  8.6 1.1 fusion.22
  9.8 0.7 convert_element_type.56
  10.5 0.7 convert_element_type.58
  11.1 6.1 %convolution_add_fusion = f32[64,2560]{1,0:T(8,128)S(1)} fusion(bf16[2048,2560]{1,0:T(8,128)(2,1)} %param.16, f32[2560]{0:T(1024)S(1)} %convert_element_type.58, bf16[64,2048]{1,0:T(8,128)(2,1)} %param.11, f32[2048]{0:T(1024)S(1)} %convert_element_type.56, f32[64]{0:T(128)S(1)} %add_rsqrt_fusion.1), kind=kOutput, calls=%fused_computation.7 | convolution fusion | flops 671776768 | bytes 11421952 | tf_op jit(solution)/shard_map/dot_general | solution.py:36
  17.4 0.1 copy.41
  17.5 0.1 slice.64
  17.7 0.1 multiply_cosine_fusion
  18.1 0.1 copy.34
  18.3 0.1 fusion.26
  18.5 0.4 copy.38
  19.0 0.4 copy.31
  19.4 25.7 %broadcast_select_fusion.1 = (bf16[64,256,2,128]{3,2,1,0:T(2,128)(2,1)}, bf16[64,256,2,128]{3,2,1,0:T(2,128)(2,1)}) fusion(bf16[64,256,2,128]{3,2,1,0:T(2,128)(2,1)} %param.13, pred[64,256]{1,0:T(8,128)(4,1)S(1)} %get-tuple-element.12, bf16[64,2,128]{2,1,0:T(2,128)(2,1)S(1)} %copy.35, bf16[64,256,2,128]{3,2,1,0:T(2,128)(2,1)} %param.14, ...), kind=kLoop, calls=%fused_computation.2 | loop fusion | flops 8388608 | bytes 33636352 | tf_op jit(solution)/shard_map/jit(_where)/select_n | solution.py:42
  45.1 5.9 %fusion.37 = (f32[64,2,8]{2,1,0:T(2,128)S(1)}, f32[64,2,8,256]{3,2,1,0:T(8,128)S(1)}) fusion(bf16[64,256,2,128]{3,2,1,0:T(2,128)(2,1)} %get-tuple-element.7, pred[64,256]{1,0:T(8,128)(4,1)S(1)} %get-tuple-element.11, bf16[64,2,8,64]{3,2,1,0:T(8,128)(2,1)S(1)} %fusion.26, bf16[64,2,8,64]{3,2,1,0:T(8,128)(2,1)S(1)} %copy.31), kind=kOutput, calls=%fused_computation.60 | convolution fusion | flops 68681984 | bytes 9719808 | tf_op jit(solution)/shard_map/sub | solution.py:47
  51.0 4.7 %fusion.17 = bf16[64,2,8,128]{3,2,1,0:T(8,128)(2,1)S(1)} fusion(bf16[64,256,2,128]{3,2,1,0:T(2,128)(2,1)} %get-tuple-element.8, f32[64,2,8,256]{3,2,1,0:T(8,128)S(1)} %get-tuple-element.14, f32[64,2,8]{2,1,0:T(2,128)S(1)} %get-tuple-element.13), kind=kOutput, calls=%fused_computation.19 | convolution fusion | flops 67764224 | bytes 9703424 | tf_op jit(solution)/shard_map/bgql,blgd->bgqd/dot_general | solution.py:48
  55.7 5.1 %multiply_reduce_fusion = (f32[64]{0:T(128)S(1)}, f32[64,2048]{1,0:T(8,128)S(1)}) fusion(bf16[2048,2048]{1,0:T(8,128)(2,1)} %param.18, bf16[8,8,16,128]{3,2,1,0:T(8,128)(2,1)S(1)} %bitcast.43, bf16[64,2048]{1,0:T(8,128)(2,1)S(1)} %copy-done), kind=kOutput, calls=%fused_computation.32 | convolution fusion | flops 537395136 | bytes 9437440 | tf_op jit(solution)/shard_map/dot_general | solution.py:50
  60.8 0.8 multiply_convert_fusion
  61.7 0.2 reduce-scatter.2.cloned.1.call-start
  61.9 16.5 %all-gather.2.cloned.1.call-done = bf16[256,2048]{1,0:T(8,128)(2,1)} async-done(((bf16[64,2048]{1,0:T(8,128)(2,1)}), bf16[256,2048]{1,0:T(8,128)(2,1)}) %all-gather.2.cloned.1.call-update) | async-done | bytes 1048592 | tf_op jit(solution)/shard_map/all_gather | solution.py:61
  78.4 11.1 %fusion.20 = f32[256,2,2752]{0,2,1:T(8,128)S(1)} fusion(bf16[2,2752,2048]{2,1,0:T(8,128)(2,1)} %param.20, bf16[256,2048]{1,0:T(8,128)(2,1)} %all-gather.2.cloned.1.call-done), kind=kOutput, calls=%fused_computation.20 | convolution fusion | flops 5771362304 | bytes 29229056 | tf_op jit(solution)/shard_map/bh,cfh->bcf/dot_general | solution.py:62
  89.5 8.6 %convolution_convert_fusion = bf16[256,2048]{1,0:T(8,128)(2,1)} fusion(bf16[2752,2048]{1,0:T(8,128)(2,1)} %param.21, f32[256,2,2752]{0,2,1:T(8,128)S(1)} %fusion.20), kind=kOutput, calls=%fused_computation.12 | convolution fusion | flops 2890432512 | bytes 17956864 | tf_op jit(solution)/shard_map/dot_general | solution.py:64
  98.1 19.3 %reduce-scatter.2.cloned.1.call-done = bf16[64,2048]{1,0:T(8,128)(2,1)} async-done(((bf16[256,2048]{1,0:T(8,128)(2,1)}), bf16[64,2048]{1,0:T(8,128)(2,1)}) %reduce-scatter.2.cloned.1.call-update) | async-done | bytes 262160 | tf_op jit(solution)/shard_map/reduce_scatter | solution.py:65
  117.4 1.7 %add_convert_fusion = bf16[64,2048]{1,0:T(8,128)(2,1)} fusion(f32[64,2048]{1,0:T(8,128)S(1)} %get-tuple-element.16, bf16[64,2048]{1,0:T(8,128)(2,1)} %reduce-scatter.2.cloned.1.call-done), kind=kLoop, calls=%fused_computation.30 | loop fusion | flops 393216 | bytes 1048576 | tf_op jit(solution)/shard_map/convert_element_type | solution.py:66
  (24 shorter events, 0.7 us)
Async XLA Ops:
  7.2 71.2 %all-gather.2.cloned.1.call-start = ((), (), s32[]{:S(2)}) async-start(), calls=%async_computation.1 | async-start | bytes 1310720 | tf_op jit(solution)/shard_map/all_gather | solution.py:61
  11.1 6.2 %copy-start.1 = (bf16[2048]{0:T(1024)(128)(2,1)S(1)}, bf16[2048]{0:T(1024)(128)(2,1)}, u32[]{:S(2)}) copy-start(bf16[2048]{0:T(1024)(128)(2,1)} %param.19) | copy-start | bytes 12292
  51.0 4.7 %copy-start = (bf16[64,2048]{1,0:T(8,128)(2,1)S(1)}, bf16[64,2048]{1,0:T(8,128)(2,1)}, u32[]{:S(2)}) copy-start(bf16[64,2048]{1,0:T(8,128)(2,1)} %param.11) | copy-start | bytes 786436
  61.7 55.7 %reduce-scatter.2.cloned.1.call-start = ((), (), s32[]{:S(2)}) async-start(), calls=%async_computation.2 | async-start | bytes 1310720 | tf_op jit(solution)/shard_map/reduce_scatter | solution.py:65
Sparse Core Ops, SparseCore 0:
  61.8 16.5 all-gather.1
  98.2 19.1 reduce-scatter.1
where the time goes:
time: 126 us
  matrix products  41.4 us (33%)
  waiting for transfers between devices  35.8 us (28%)
  other arithmetic  32.7 us (26%)
  between operations  14.3 us (11%)
  local copies, waits for them, and re-layouts  1.42 us (1%)
    select_n x1, other arithmetic, attention_block(): k_out = jnp.where(at_len, key_new[:, None], k_cache)  25.7 us
    reduce_scatter x1, waiting for transfers between devices, local_layer(): mlp_out = lax.psum_scatter(part_sum, 'grp', scatter_dimension=0, tiled=True)  19.3 us
    all_gather x1, waiting for transfers between devices, local_layer(): group_rows = lax.all_gather(mlp_in, 'grp', axis=0, tiled=True)  16.5 us
    dot_general x1, matrix products, local_layer(): jnp.einsum('bh,cfh->bcf', group_rows, w_in, preferred_element_type=jnp.fl...  11.1 us
    dot_general x1, matrix products, local_layer(): jnp.dot(swiglu, w_out, preferred_element_type=jnp.float32)  8.56 us
    dot_general x1, matrix products, attention_block(): jnp.dot(normed, w_qkv, preferred_element_type=jnp.float32)  6.1 us
    sub x1, matrix products, attention_block(): jax.nn.softmax(jnp.where(visible, attn_scores, -jnp.inf), axis=-1)  5.9 us
    dot_general x1, matrix products, attention_block(): jnp.dot(context, w_proj, preferred_element_type=jnp.float32)  5.09 us
  transfers between devices with their start and end apart: 2, of which 2 were waited for; matrix products, arithmetic and copies ran while one was open for 0% of the time, Pallas kernels for 0%

commit v1 on v0

v1 whole, which is shorter than its diff:
```python
import jax
import jax.numpy as jnp
from jax import lax
from jax.experimental import pallas as pl
from jax.experimental.pallas import tpu as pltpu
from jax.sharding import PartitionSpec as P

HEAD_DIM = 128
ROPE_BASE = 10000.0
EPS = 1e-5
HIDDEN = 2048
HEADS = 16
KV = 2
ROWS = 64
LMAX = 256
FLAT = LMAX * KV
FFN_LOC = 2752
QKV_CHUNK = 512
N_QKV = 5
PROJ_CHUNK = 512
N_PROJ = 4
SEQ_CHUNK = 8
N_SEQ = ROWS // SEQ_CHUNK
SUB = 4
F_CHUNK = 256
N_F = 11
D_CHUNK = 256
N_D = HIDDEN // D_CHUNK
AG_PIECES = 4
AG_ROWS = ROWS // AG_PIECES
LAG = 6
F32 = jnp.float32
BF16 = jnp.bfloat16


def attn_kernel(len_ref, x_ref, cos_ref, sin_ref, ga_ref, gm_ref, b_ref, wqkv_hbm, k_hbm, v_hbm, wproj_hbm,
                h_ref, m_ref, kout_hbm, vout_hbm,
                wq_buf, wp_buf, k_buf, v_buf, q_scr, kn_scr, vn_scr, ctx_scr, act_buf,
                wq_sem, wp_sem, k_sem, v_sem, ko_sem, vo_sem):
    def wq_copy(c):
        return pltpu.make_async_copy(wqkv_hbm.at[:, pl.ds(c * QKV_CHUNK, QKV_CHUNK)], wq_buf.at[c], wq_sem.at[c])

    def wp_copy(c):
        return pltpu.make_async_copy(wproj_hbm.at[:, pl.ds(c * PROJ_CHUNK, PROJ_CHUNK)], wp_buf.at[c], wp_sem.at[c])

    def k_copy(i):
        rows = pl.ds(i * SEQ_CHUNK, SEQ_CHUNK)
        return pltpu.make_async_copy(k_hbm.at[rows], k_buf.at[rows], k_sem.at[i])

    def v_copy(i):
        rows = pl.ds(i * SEQ_CHUNK, SEQ_CHUNK)
        return pltpu.make_async_copy(v_hbm.at[rows], v_buf.at[rows], v_sem.at[i])

    def ko_copy(i):
        rows = pl.ds(i * SEQ_CHUNK, SEQ_CHUNK)
        return pltpu.make_async_copy(k_buf.at[rows], kout_hbm.at[rows], ko_sem.at[i])

    def vo_copy(i):
        rows = pl.ds(i * SEQ_CHUNK, SEQ_CHUNK)
        return pltpu.make_async_copy(v_buf.at[rows], vout_hbm.at[rows], vo_sem.at[i])

    for c in range(N_QKV):
        wq_copy(c).start()
    for i in range(N_SEQ):
        k_copy(i).start()
        v_copy(i).start()
    for c in range(N_PROJ):
        wp_copy(c).start()

    x = x_ref[...].astype(F32)
    inv = lax.rsqrt(jnp.mean(x * x, axis=-1, keepdims=True) + EPS)
    act_buf[...] = (x * inv * ga_ref[...]).astype(BF16)
    normed = act_buf[...]
    cosine = cos_ref[...]
    sine = sin_ref[...]
    even = (lax.broadcasted_iota(jnp.int32, (ROWS, HEAD_DIM), 1) % 2) == 0

    def rotate(v):
        swapped = jnp.where(even, pltpu.roll(v, HEAD_DIM - 1, 1), pltpu.roll(v, 1, 1))
        return v * cosine + swapped * sine

    for c in range(N_QKV):
        wq_copy(c).wait()
        cols = pl.ds(c * QKV_CHUNK, QKV_CHUNK)
        acc = jnp.dot(normed, wq_buf[c], preferred_element_type=F32) + b_ref[:, cols]
        for t in range(QKV_CHUNK // HEAD_DIM):
            head = c * (QKV_CHUNK // HEAD_DIM) + t
            part = acc[:, t * HEAD_DIM:(t + 1) * HEAD_DIM]
            if head < HEADS:
                q_scr[pl.ds(head, ROWS, stride=HEADS), :] = rotate(part)
            elif head < HEADS + KV:
                kn_scr[head - HEADS] = rotate(part)
            else:
                vn_scr[head - HEADS - KV] = part

    row16 = lax.broadcasted_iota(jnp.int32, (16, HEAD_DIM), 0)
    col = lax.broadcasted_iota(jnp.int32, (HEADS, FLAT), 1)
    head_row = lax.broadcasted_iota(jnp.int32, (HEADS, FLAT), 0)
    pos = jnp.where((col % KV) == (head_row // (HEADS // KV)), col // KV, 2 * LMAX)

    def chunk_body(i, carry):
        k_copy(i).wait()
        v_copy(i).wait()
        for u in range(SEQ_CHUNK):
            b = i * SEQ_CHUNK + u
            ln = len_ref[b]
            base = pl.multiple_of((ln // 8) * 16, 16)
            hit = (row16 // 2) == (ln % 8)
            for buf, new in ((k_buf, kn_scr), (v_buf, vn_scr)):
                fresh = jnp.where(row16 % 2 == 0, new[0, pl.ds(b, 1), :], new[1, pl.ds(b, 1), :])
                old = buf[b, pl.ds(base, 16), :].astype(F32)
                buf[b, pl.ds(base, 16), :] = jnp.where(hit, fresh, old).astype(BF16)
        for s0 in range(0, SEQ_CHUNK, SUB):
            probs = []
            for u in range(s0, s0 + SUB):
                b = i * SEQ_CHUNK + u
                q = q_scr[pl.ds(pl.multiple_of(b * HEADS, HEADS), HEADS), :].astype(BF16)
                s = lax.dot_general(q, k_buf[b], (((1,), (1,)), ((), ())), preferred_element_type=F32)
                s = jnp.where(pos <= len_ref[b], s * (HEAD_DIM ** -0.5), -jnp.inf)
                e = jnp.exp(s - jnp.max(s, axis=1, keepdims=True))
                probs.append((e / jnp.sum(e, axis=1, keepdims=True)).astype(BF16))
            for u in range(s0, s0 + SUB):
                b = i * SEQ_CHUNK + u
                ctx_scr[pl.ds(pl.multiple_of(b * HEADS, HEADS), HEADS), :] = jnp.dot(
                    probs[u - s0], v_buf[b], preferred_element_type=F32)
        ko_copy(i).start()
        vo_copy(i).start()
        return carry

    lax.fori_loop(0, N_SEQ, chunk_body, 0)

    for h in range(HEADS):
        act_buf[:, h * HEAD_DIM:(h + 1) * HEAD_DIM] = ctx_scr[pl.ds(h, ROWS, stride=HEADS), :].astype(BF16)
    ctx = act_buf[...]
    total = jnp.zeros((ROWS, 1), F32)
    for c in range(N_PROJ):
        wp_copy(c).wait()
        cols = slice(c * PROJ_CHUNK, (c + 1) * PROJ_CHUNK)
        hid = x_ref[:, cols].astype(F32) + jnp.dot(ctx, wp_buf[c], preferred_element_type=F32)
        h_ref[:, cols] = hid
        total = total + jnp.sum(hid * hid, axis=-1, keepdims=True)
    inv2 = lax.rsqrt(total * (1.0 / HIDDEN) + EPS)
    for c in range(N_PROJ):
        cols = slice(c * PROJ_CHUNK, (c + 1) * PROJ_CHUNK)
        m_ref[:, cols] = (h_ref[:, cols] * inv2 * gm_ref[:, cols]).astype(BF16)
    for i in range(N_SEQ):
        ko_copy(i).wait()
        vo_copy(i).wait()


def attention(lens, x, cosine, sine, ga, gm, bias, w_qkv, k_flat, v_flat, w_proj):
    vmem = pl.BlockSpec(memory_space=pltpu.VMEM)
    hbm = pl.BlockSpec(memory_space=pl.ANY)
    smem = pl.BlockSpec(memory_space=pltpu.SMEM)
    dma = pltpu.SemaphoreType.DMA
    return pl.pallas_call(
        attn_kernel,
        out_shape=(jax.ShapeDtypeStruct((ROWS, HIDDEN), F32), jax.ShapeDtypeStruct((ROWS, HIDDEN), BF16),
                   jax.ShapeDtypeStruct(k_flat.shape, BF16), jax.ShapeDtypeStruct(v_flat.shape, BF16)),
        in_specs=[smem] + [vmem] * 6 + [hbm] * 4,
        out_specs=(vmem, vmem, hbm, hbm),
        scratch_shapes=[
            pltpu.VMEM((N_QKV, HIDDEN, QKV_CHUNK), BF16),
            pltpu.VMEM((N_PROJ, HIDDEN, PROJ_CHUNK), BF16),
            pltpu.VMEM((ROWS, FLAT, HEAD_DIM), BF16),
            pltpu.VMEM((ROWS, FLAT, HEAD_DIM), BF16),
            pltpu.VMEM((ROWS * HEADS, HEAD_DIM), F32),
            pltpu.VMEM((KV, ROWS, HEAD_DIM), F32),
            pltpu.VMEM((KV, ROWS, HEAD_DIM), F32),
            pltpu.VMEM((ROWS * HEADS, HEAD_DIM), F32),
            pltpu.VMEM((ROWS, HIDDEN), BF16),
            dma((N_QKV,)), dma((N_PROJ,)), dma((N_SEQ,)), dma((N_SEQ,)), dma((N_SEQ,)), dma((N_SEQ,)),
        ],
        compiler_params=pltpu.CompilerParams(vmem_limit_bytes=60 * 1024 * 1024),
        name="attn_block",
    )(lens, x, cosine, sine, ga, gm, bias, w_qkv, k_flat, v_flat, w_proj)


def mlp_kernel(m_ref, h_ref, win_hbm, wout_hbm, y_ref,
               rows_buf, win_buf, wout_buf, g_buf, pair_send, pair_recv, near_send, near_recv, far_keep, far_send, far_recv,
               own_acc, win_sem, wout_sem, agx_s, agx_r, agp_s, agp_r, agr_s, agr_r,
               ps_s, ps_r, ns_s, ns_r, fs_s, fs_r):
    me = lax.axis_index('grp')
    partner = me + 1 - 2 * (me % 2)
    cross = (me + 2) % 4

    def win_copy(i, part, width):
        rows = pl.ds(i * F_CHUNK, width)
        return pltpu.make_async_copy(win_hbm.at[part, rows], win_buf.at[part, rows], win_sem.at[part, i])

    def wout_copy(j):
        cols = pl.ds(j * D_CHUNK, D_CHUNK)
        return pltpu.make_async_copy(wout_hbm.at[:, cols], wout_buf.at[:, cols], wout_sem.at[j])

    tail = FFN_LOC - (N_F - 1) * F_CHUNK
    widths = [F_CHUNK] * (N_F - 1) + [tail]
    for i in range(N_F):
        for part in range(2):
            win_copy(i, part, widths[i]).start()
    for j in range(N_D):
        wout_copy(j).start()

    barrier = pltpu.get_barrier_semaphore()
    for peer in (partner, cross):
        pl.semaphore_signal(barrier, inc=1, device_id={'grp': peer}, device_id_type=pl.DeviceIdType.MESH)
    pl.semaphore_wait(barrier, 2)

    def send(src, dst, ssem, rsem, peer):
        return pltpu.make_async_remote_copy(src_ref=src, dst_ref=dst, send_sem=ssem, recv_sem=rsem,
                                            device_id={'grp': peer}, device_id_type=pl.DeviceIdType.MESH)

    cross_copies = [send(m_ref.at[pl.ds(p * AG_ROWS, AG_ROWS)], rows_buf.at[pl.ds(2 * ROWS + p * AG_ROWS, AG_ROWS)],
                         agx_s.at[p], agx_r.at[p], cross) for p in range(AG_PIECES)]
    for cp in cross_copies:
        cp.start()
    pair_copy = send(m_ref, rows_buf.at[pl.ds(ROWS, ROWS)], agp_s, agp_r, partner)
    pair_copy.start()
    rows_buf[pl.ds(0, ROWS), :] = m_ref[...]
    relays = []
    for p in range(AG_PIECES):
        cross_copies[p].wait_recv()
        relay = send(rows_buf.at[pl.ds(2 * ROWS + p * AG_ROWS, AG_ROWS)],
                     rows_buf.at[pl.ds(3 * ROWS + p * AG_ROWS, AG_ROWS)], agr_s.at[p], agr_r.at[p], partner)
        relay.start()
        relays.append(relay)
    pair_copy.wait()
    for p in range(AG_PIECES):
        cross_copies[p].wait_send()
        relays[p].wait()

    def ffn_chunk(i, width):
        for part in range(2):
            win_copy(i, part, width).wait()
        fr = pl.ds(pl.multiple_of(i * F_CHUNK, F_CHUNK), width)
        rows = rows_buf[...]
        dims = (((1,), (1,)), ((), ()))
        gate = lax.dot_general(rows, win_buf[0, fr, :], dims, preferred_element_type=F32)
        up = lax.dot_general(rows, win_buf[1, fr, :], dims, preferred_element_type=F32)
        g_buf[:, fr] = (gate * jax.nn.sigmoid(gate) * up).astype(BF16)

    lax.fori_loop(0, N_F - 1, lambda i, c: (ffn_chunk(i, F_CHUNK), c)[1], 0)
    ffn_chunk(N_F - 1, tail)

    pair_copies = [send(pair_send.at[j], pair_recv.at[j], ps_s.at[j], ps_r.at[j], partner) for j in range(N_D)]
    near_copies = [send(near_send.at[j], near_recv.at[j], ns_s.at[j], ns_r.at[j], partner) for j in range(N_D)]
    far_copies = [send(far_send.at[j], far_recv.at[j], fs_s.at[j], fs_r.at[j], cross) for j in range(N_D)]

    for step in range(2 * N_D + 2):
        if 1 <= step <= N_D:
            pair_copies[step - 1].start()
        elif N_D < step <= 2 * N_D:
            near_copies[step - 1 - N_D].start()
        if LAG + 1 <= step <= LAG + N_D:
            far_copies[step - LAG - 1].start()
        if step < N_D:
            wout_copy(step).wait()
            cols = slice(step * D_CHUNK, (step + 1) * D_CHUNK)
            part = jnp.dot(g_buf[2 * ROWS:, :], wout_buf[:, cols], preferred_element_type=F32)
            far_keep[step] = part[:ROWS]
            pair_send[step] = part[ROWS:].astype(BF16)
        elif step < 2 * N_D:
            j = step - N_D
            cols = slice(j * D_CHUNK, (j + 1) * D_CHUNK)
            part = jnp.dot(g_buf[:2 * ROWS, :], wout_buf[:, cols], preferred_element_type=F32)
            own_acc[j] = part[:ROWS] + h_ref[:, cols]
            near_send[j] = part[ROWS:].astype(BF16)
        if LAG <= step < LAG + N_D:
            j = step - LAG
            pair_copies[j].wait_recv()
            far_send[j] = (far_keep[j] + pair_recv[j].astype(F32)).astype(BF16)

    for j in range(N_D):
        cols = slice(j * D_CHUNK, (j + 1) * D_CHUNK)
        near_copies[j].wait_recv()
        far_copies[j].wait_recv()
        y_ref[:, cols] = (own_acc[j] + near_recv[j].astype(F32) + far_recv[j].astype(F32)).astype(BF16)
    for j in range(N_D):
        pair_copies[j].wait_send()
        near_copies[j].wait_send()
        far_copies[j].wait_send()


def mlp(m, h, w_in, w_out):
    vmem = pl.BlockSpec(memory_space=pltpu.VMEM)
    hbm = pl.BlockSpec(memory_space=pl.ANY)
    dma = pltpu.SemaphoreType.DMA
    piece = (N_D, ROWS, D_CHUNK)
    return pl.pallas_call(
        mlp_kernel,
        out_shape=jax.ShapeDtypeStruct((ROWS, HIDDEN), BF16),
        in_specs=[vmem, vmem, hbm, hbm],
        out_specs=vmem,
        scratch_shapes=[
            pltpu.VMEM((4 * ROWS, HIDDEN), BF16),
            pltpu.VMEM((2, FFN_LOC, HIDDEN), BF16),
            pltpu.VMEM((FFN_LOC, HIDDEN), BF16),
            pltpu.VMEM((4 * ROWS, FFN_LOC), BF16),
            pltpu.VMEM(piece, BF16), pltpu.VMEM(piece, BF16),
            pltpu.VMEM(piece, BF16), pltpu.VMEM(piece, BF16),
            pltpu.VMEM(piece, F32), pltpu.VMEM(piece, BF16), pltpu.VMEM(piece, BF16),
            pltpu.VMEM(piece, F32),
            dma((2, N_F)), dma((N_D,)),
            dma((AG_PIECES,)), dma((AG_PIECES,)), dma, dma, dma((AG_PIECES,)), dma((AG_PIECES,)),
            dma((N_D,)), dma((N_D,)), dma((N_D,)), dma((N_D,)), dma((N_D,)), dma((N_D,)),
        ],
        compiler_params=pltpu.CompilerParams(vmem_limit_bytes=60 * 1024 * 1024, collective_id=0, has_side_effects=True),
        name="mlp_block",
    )(m, h, w_in, w_out)


def rope_tables(lens):
    rot = HEAD_DIM // 2
    lane = jnp.arange(HEAD_DIM)
    inv_freq = ROPE_BASE ** (-(2 * (lane // 2)).astype(F32) / rot)
    angles = lens.astype(F32)[:, None] * inv_freq[None, :]
    active = lane[None, :] < rot
    sign = jnp.where(lane % 2 == 0, -1.0, 1.0)[None, :]
    return jnp.where(active, jnp.cos(angles), 1.0), jnp.where(active, jnp.sin(angles) * sign, 0.0)


def solution(mesh):
    row_spec = P(('rep', 'grp'))
    repl_spec = P()

    def local_layer(x_in, seq_len, k_cache, v_cache, gamma_attn, w_qkv, b_qkv, w_proj, gamma_mlp, w_in, w_out):
        cosine, sine = rope_tables(seq_len)
        ga = gamma_attn.astype(F32)[None, :]
        gm = gamma_mlp.astype(F32)[None, :]
        bias = b_qkv.astype(F32)[None, :]
        k_flat = k_cache.reshape(ROWS, FLAT, HEAD_DIM)
        v_flat = v_cache.reshape(ROWS, FLAT, HEAD_DIM)
        h, m, k_out, v_out = attention(seq_len, x_in, cosine, sine, ga, gm, bias, w_qkv, k_flat, v_flat, w_proj)
        layer_out = mlp(m, h, w_in, w_out)
        return layer_out, k_out.reshape(k_cache.shape), v_out.reshape(v_cache.shape)

    return jax.shard_map(local_layer, mesh=mesh,
                         in_specs=(row_spec, row_spec, row_spec, row_spec, repl_spec, repl_spec, repl_spec,
                                   repl_spec, repl_spec, P(None, 'grp', None), P('grp', None)),
                         out_specs=(row_spec, row_spec, row_spec), check_vma=False)
```

time: 126 us -> 65.4 us (0.52)
  Pallas kernels: 0 us -> 57.5 us
  matrix products: 41.4 us -> 0 us
  waiting for transfers between devices: 35.8 us -> 0 us
  other arithmetic: 32.7 us -> 4.05 us
  between operations: 14.3 us -> 0.65 us
  local copies, waits for them, and re-layouts: 1.42 us -> 2.96 us
    pallas_call x0 -> x2, Pallas kernels: none -> 57.5 us  [the longest x1 33.8 us: mlp(): pl.pallas_call(mlp_kernel, out_shape=jax.ShapeDtypeStruct((ROWS, HIDDEN),...]
    dot_general x5 -> x0, matrix products: 35.5 us -> none  [the longest x1 11.1 us: local_layer(): jnp.einsum('bh,cfh->bcf', group_rows, w_in, preferred_element_type=jnp.fl...]
    select_n x1 -> x2, other arithmetic: 25.7 us -> 0.84 us  [the longest x1 0.83 us: rope_tables(): jnp.where(active, jnp.sin(angles) * sign, 0.0)]
    reduce_scatter x1 -> x0, waiting for transfers between devices: 19.3 us -> none  [local_layer(): mlp_out = lax.psum_scatter(part_sum, 'grp', scatter_dimension=0, tiled=True)]
    all_gather x1 -> x0, waiting for transfers between devices: 16.5 us -> none  [local_layer(): group_rows = lax.all_gather(mlp_in, 'grp', axis=0, tiled=True)]
    sub x1 -> x0, matrix products: 5.9 us -> none  [attention_block(): jax.nn.softmax(jnp.where(visible, attn_scores, -jnp.inf), axis=-1)]
    convert_element_type x6 -> x1, other arithmetic: 4.58 us -> 0.66 us  [rope_tables(): angles = lens.astype(F32)[:, None] * inv_freq[None, :]]
    broadcast_in_dim x0 -> x2, other arithmetic: none -> 2.55 us  [the longest x1 1.28 us: local_layer(): gm = gamma_mlp.astype(F32)[None, :]]
  transfers between devices with their start and end apart: 2 -> 0, of which waited for: 2 -> 0; matrix products, arithmetic and copies ran while one was open for 0% -> 0% of each run, Pallas kernels for 0% -> 0%
where the time goes in v1:
time: 65.4 us; the launch traced here: 65.1 us
  Pallas kernels  57.5 us (88%)
  other arithmetic  4.05 us (6%)
  local copies, waits for them, and re-layouts  2.96 us (5%)
    pallas_call x1, Pallas kernels, mlp(): pl.pallas_call(mlp_kernel, out_shape=jax.ShapeDtypeStruct((ROWS, HIDDEN),...  33.8 us
    pallas_call x1, Pallas kernels, attention(): pl.pallas_call(attn_kernel, out_shape=(jax.ShapeDtypeStruct((ROWS, HIDDEN...  23.7 us
    unnamed x1, local copies, waits for them, and re-layouts  1.67 us

profile of v1, /device:TPU:0, one launch (start us, length us, event | category | flops | bytes accessed | tf_op | source)
XLA Modules:
  0.0 65.1 jit_solution(13659119377924078126)
XLA Ops:
  0.6 0.7 %convert_element_type.13 = f32[64]{0:T(128)S(1)} convert(s32[64]{0:T(128)} %len_ref.1) | non-fusion elementwise | flops 64 | bytes 512 | tf_op jit(solution)/shard_map/convert_element_type | solution.py:315
  1.3 1.3 %broadcast_in_dim.58 = f32[2048]{0:T(1024)} convert(bf16[2048]{0:T(1024)(128)(2,1)} %param.15) | non-fusion elementwise | flops 2048 | bytes 12288 | tf_op jit(solution)/shard_map/broadcast_in_dim | solution.py:327
  2.6 1.3 %broadcast_in_dim.59 = f32[2048]{0:T(1024)} convert(bf16[2048]{0:T(1024)(128)(2,1)} %param.19) | non-fusion elementwise | flops 2048 | bytes 12288 | tf_op jit(solution)/shard_map/broadcast_in_dim | solution.py:328
  3.9 1.3 %reshape.59.b_ref = f32[1,2560]{1,0:T(1,128)} reshape(bf16[2560]{0:T(1024)(128)(2,1)} %param.17) | data formatting | bytes 15360 | tf_op jit(solution)/shard_map/broadcast_in_dim | solution.py:329
  5.1 0.8 %fusion.2 = (f32[64,128]{1,0:T(8,128)}, f32[64,128]{1,0:T(8,128)}) fusion(f32[128]{0:T(128)S(1)} %get-tuple-element.13, f32[128]{0:T(128)S(1)} %get-tuple-element.14, f32[64]{0:T(128)S(1)} %convert_element_type.13, pred[128]{0:T(512)(128)(4,1)S(1)} %iota_compare_fusion), kind=kLoop, calls=%fused_computation.4 | loop fusion | flops 32768 | bytes 66944 | tf_op jit(solution)/shard_map/jit(_where)/select_n | solution.py:318
  6.0 23.7 %attn_block.1 = (f32[64,2048]{1,0:T(8,128)}, bf16[64,2048]{1,0:T(8,128)(2,1)}, bf16[64,512,128]{2,1,0:T(8,128)(2,1)}, bf16[64,512,128]{2,1,0:T(8,128)(2,1)}) custom-call(s32[64]{0:T(128)} %len_ref.1, bf16[64,2048]{1,0:T(8,128)(2,1)} %x_ref.1, f32[64,128]{1,0:T(8,128)} %get-tuple-element.12.cos_ref, f32[64,128]{1,0:T(8,128)} %get-tuple-element.11.sin_ref, ...), custom_call_target="tpu_custom_call" | custom-call | tf_op jit(solution)/shard_map/attn_block/pallas_call | solution.py:156
  29.7 33.8 %mlp_block.1 = bf16[64,2048]{1,0:T(8,128)(2,1)} custom-call(bf16[64,2048]{1,0:T(8,128)(2,1)} %get-tuple-element.7.m_ref, f32[64,2048]{1,0:T(8,128)} %get-tuple-element.8.h_ref, bf16[2,2752,2048]{2,1,0:T(8,128)(2,1)} %win_hbm.1, bf16[2752,2048]{1,0:T(8,128)(2,1)} %wout_hbm.1), custom_call_target="tpu_custom_call" | custom-call | tf_op jit(solution)/shard_map/mlp_block/pallas_call | solution.py:288
  63.5 1.7 %copy.15 = bf16[64,2048]{1,0:T(8,128)(2,1)} copy(bf16[64,2048]{1,0:T(8,128)(2,1)} %mlp_block.1) | data formatting | bytes 524288
  (2 shorter events, 0.0 us)

commit v2 on v1

v2 whole, which is shorter than its diff:
```python
import jax
import jax.numpy as jnp
import numpy as np
from jax import lax
from jax.experimental import pallas as pl
from jax.experimental.pallas import tpu as pltpu
from jax.sharding import PartitionSpec as P

HEAD_DIM = 128
ROPE_BASE = 10000.0
EPS = 1e-5
HIDDEN = 2048
HEADS = 16
KV = 2
ROWS = 64
LMAX = 256
FLAT = LMAX * KV
FFN_LOC = 2752
QKV_CHUNK = 512
N_QKV = 5
PROJ_CHUNK = 512
N_PROJ = 4
SEQ_CHUNK = 8
N_SEQ = ROWS // SEQ_CHUNK
SUB = 8
WINDOW = 7
F_CHUNK = 256
N_F = 11
D_CHUNK = 256
N_D = HIDDEN // D_CHUNK
AG_PIECES = 4
AG_ROWS = ROWS // AG_PIECES
LAG = 6
F32 = jnp.float32
BF16 = jnp.bfloat16


def attn_kernel(len_ref, freq_hbm, x_hbm, ga_hbm, gm_hbm, b_hbm, wqkv_hbm, k_hbm, v_hbm, wproj_hbm,
                h_hbm, m_hbm, kout_hbm, vout_hbm,
                freq_ref, x_ref, ga_ref, gm_ref, b_ref, h_ref, m_ref,
                wq_buf, wp_buf, k_buf, v_buf, q_scr, kn_scr, vn_scr, ctx_scr, act_buf,
                small_sem, wq_sem, wp_sem, k_sem, v_sem, ko_sem, vo_sem, out_sem):
    small = [pltpu.make_async_copy(src, dst, small_sem.at[n]) for n, (src, dst) in enumerate(
        ((x_hbm, x_ref), (ga_hbm, ga_ref), (freq_hbm, freq_ref), (b_hbm, b_ref), (gm_hbm, gm_ref)))]

    def wq_copy(c):
        return pltpu.make_async_copy(wqkv_hbm.at[:, pl.ds(c * QKV_CHUNK, QKV_CHUNK)], wq_buf.at[c], wq_sem.at[c])

    def wp_copy(c):
        return pltpu.make_async_copy(wproj_hbm.at[:, pl.ds(c * PROJ_CHUNK, PROJ_CHUNK)], wp_buf.at[c], wp_sem.at[c])

    def k_copy(i):
        rows = pl.ds(i * SEQ_CHUNK, SEQ_CHUNK)
        return pltpu.make_async_copy(k_hbm.at[rows], k_buf.at[rows], k_sem.at[i])

    def v_copy(i):
        rows = pl.ds(i * SEQ_CHUNK, SEQ_CHUNK)
        return pltpu.make_async_copy(v_hbm.at[rows], v_buf.at[rows], v_sem.at[i])

    def ko_copy(i):
        rows = pl.ds(i * SEQ_CHUNK, SEQ_CHUNK)
        return pltpu.make_async_copy(k_buf.at[rows], kout_hbm.at[rows], ko_sem.at[i])

    def vo_copy(i):
        rows = pl.ds(i * SEQ_CHUNK, SEQ_CHUNK)
        return pltpu.make_async_copy(v_buf.at[rows], vout_hbm.at[rows], vo_sem.at[i])

    for cp in small:
        cp.start()
    def fetch(n):
        if n < N_QKV:
            wq_copy(n).start()
        elif n < N_QKV + N_SEQ:
            k_copy(n - N_QKV).start()
            v_copy(n - N_QKV).start()
        elif n < N_QKV + N_SEQ + N_PROJ:
            wp_copy(n - N_QKV - N_SEQ).start()

    for n in range(WINDOW):
        fetch(n)

    for cp in small:
        cp.wait()
    x = x_ref[...].astype(F32)
    inv = lax.rsqrt(jnp.mean(x * x, axis=-1, keepdims=True) + EPS)
    act_buf[...] = (x * inv * ga_ref[...].astype(F32).reshape(1, HIDDEN)).astype(BF16)
    normed = act_buf[...]
    sub = lax.broadcasted_iota(jnp.int32, (8, HEAD_DIM), 0)
    tiles = []
    for t in range(ROWS // 8):
        tile = jnp.zeros((8, HEAD_DIM), jnp.int32)
        for r in range(8):
            tile = jnp.where(sub == r, len_ref[t * 8 + r], tile)
        tiles.append(tile)
    angles = jnp.concatenate(tiles, axis=0).astype(F32) * freq_ref[...]
    lane = lax.broadcasted_iota(jnp.int32, (ROWS, HEAD_DIM), 1)
    even = (lane % 2) == 0
    turned = lane < HEAD_DIM // 2
    cosine = jnp.where(turned, jnp.cos(angles), 1.0)
    sine = jnp.sin(angles)
    sine = jnp.where(turned, jnp.where(even, -sine, sine), 0.0)
    bias = b_ref[...].astype(F32).reshape(1, HIDDEN + 2 * KV * HEAD_DIM)

    def rotate(v):
        swapped = jnp.where(even, pltpu.roll(v, HEAD_DIM - 1, 1), pltpu.roll(v, 1, 1))
        return v * cosine + swapped * sine

    for c in range(N_QKV):
        wq_copy(c).wait()
        fetch(c + WINDOW)
        acc = jnp.dot(normed, wq_buf[c], preferred_element_type=F32) + bias[:, c * QKV_CHUNK:(c + 1) * QKV_CHUNK]
        for t in range(QKV_CHUNK // HEAD_DIM):
            head = c * (QKV_CHUNK // HEAD_DIM) + t
            part = acc[:, t * HEAD_DIM:(t + 1) * HEAD_DIM]
            if head < HEADS:
                q_scr[pl.ds(head, ROWS, stride=HEADS), :] = rotate(part)
            elif head < HEADS + KV:
                kn_scr[head - HEADS] = rotate(part)
            else:
                vn_scr[head - HEADS - KV] = part

    row16 = lax.broadcasted_iota(jnp.int32, (16, HEAD_DIM), 0)
    col = lax.broadcasted_iota(jnp.int32, (HEADS, FLAT), 1)
    row32 = lax.broadcasted_iota(jnp.int32, (2 * HEADS, HEAD_DIM), 0)
    head_row = lax.broadcasted_iota(jnp.int32, (HEADS, FLAT), 0)
    pos = jnp.where((col % KV) == (head_row // (HEADS // KV)), col // KV, 2 * LMAX)

    def chunk_body(i, carry):
        k_copy(i).wait()
        v_copy(i).wait()

        @pl.when(i + WINDOW < N_SEQ)
        def _():
            k_copy(i + WINDOW).start()
            v_copy(i + WINDOW).start()

        @pl.when(jnp.logical_and(i + WINDOW >= N_SEQ, i + WINDOW < N_SEQ + N_PROJ))
        def _():
            wp_copy(i + WINDOW - N_SEQ).start()

        for u in range(SEQ_CHUNK):
            b = i * SEQ_CHUNK + u
            ln = len_ref[b]
            base = pl.multiple_of((ln // 8) * 16, 16)
            hit = (row16 // 2) == (ln % 8)
            for buf, new in ((k_buf, kn_scr), (v_buf, vn_scr)):
                fresh = jnp.where(row16 % 2 == 0, new[0, pl.ds(b, 1), :], new[1, pl.ds(b, 1), :])
                old = buf[b, pl.ds(base, 16), :].astype(F32)
                buf[b, pl.ds(base, 16), :] = jnp.where(hit, fresh, old).astype(BF16)
        for s0 in range(0, SEQ_CHUNK, SUB):
            probs = []
            for u in range(s0, s0 + SUB, 2):
                b = i * SEQ_CHUNK + u
                q = q_scr[pl.ds(pl.multiple_of(b * HEADS, 2 * HEADS), 2 * HEADS), :]
                first = row32 < HEADS
                q2 = jnp.concatenate([jnp.where(first, q, 0.0), jnp.where(first, 0.0, q)], axis=1).astype(BF16)
                k2 = jnp.concatenate([k_buf[b], k_buf[b + 1]], axis=1)
                s2 = lax.dot_general(q2, k2, (((1,), (1,)), ((), ())), preferred_element_type=F32)
                pair = []
                for t in range(2):
                    s = jnp.where(pos <= len_ref[b + t], s2[t * HEADS:(t + 1) * HEADS], -jnp.inf)
                    e = jnp.exp((s - jnp.max(s, axis=1, keepdims=True)) * (HEAD_DIM ** -0.5))
                    pair.append((e * (1.0 / jnp.sum(e, axis=1, keepdims=True))).astype(BF16))
                probs.append(jnp.concatenate(pair, axis=0))
            for u in range(s0, s0 + SUB, 2):
                b = i * SEQ_CHUNK + u
                v2 = jnp.concatenate([v_buf[b], v_buf[b + 1]], axis=1)
                c2 = jnp.dot(probs[(u - s0) // 2], v2, preferred_element_type=F32)
                at = pl.multiple_of(b * HEADS, 2 * HEADS)
                ctx_scr[pl.ds(at, HEADS), :] = c2[:HEADS, :HEAD_DIM]
                ctx_scr[pl.ds(at + HEADS, HEADS), :] = c2[HEADS:, HEAD_DIM:]
        ko_copy(i).start()
        vo_copy(i).start()
        return carry

    lax.fori_loop(0, N_SEQ, chunk_body, 0)

    for h in range(HEADS):
        act_buf[:, h * HEAD_DIM:(h + 1) * HEAD_DIM] = ctx_scr[pl.ds(h, ROWS, stride=HEADS), :].astype(BF16)
    ctx = act_buf[...]
    total = jnp.zeros((ROWS, 1), F32)
    for c in range(N_PROJ):
        wp_copy(c).wait()
        cols = slice(c * PROJ_CHUNK, (c + 1) * PROJ_CHUNK)
        hid = x_ref[:, cols].astype(F32) + jnp.dot(ctx, wp_buf[c], preferred_element_type=F32)
        h_ref[:, cols] = hid
        total = total + jnp.sum(hid * hid, axis=-1, keepdims=True)
    inv2 = lax.rsqrt(total * (1.0 / HIDDEN) + EPS)
    m_ref[...] = (h_ref[...] * inv2 * gm_ref[...].astype(F32).reshape(1, HIDDEN)).astype(BF16)
    h_copy = pltpu.make_async_copy(h_ref, h_hbm, out_sem.at[0])
    m_copy = pltpu.make_async_copy(m_ref, m_hbm, out_sem.at[1])
    h_copy.start()
    m_copy.start()
    for i in range(N_SEQ):
        ko_copy(i).wait()
        vo_copy(i).wait()
    h_copy.wait()
    m_copy.wait()


def attention(lens, freq, x, ga, gm, bias, w_qkv, k_flat, v_flat, w_proj):
    hbm = pl.BlockSpec(memory_space=pl.ANY)
    smem = pl.BlockSpec(memory_space=pltpu.SMEM)
    dma = pltpu.SemaphoreType.DMA
    return pl.pallas_call(
        attn_kernel,
        out_shape=(jax.ShapeDtypeStruct((ROWS, HIDDEN), F32), jax.ShapeDtypeStruct((ROWS, HIDDEN), BF16),
                   jax.ShapeDtypeStruct(k_flat.shape, BF16), jax.ShapeDtypeStruct(v_flat.shape, BF16)),
        in_specs=[smem] + [hbm] * 9,
        out_specs=(hbm,) * 4,
        scratch_shapes=[
            pltpu.VMEM((1, HEAD_DIM), F32), pltpu.VMEM((ROWS, HIDDEN), BF16), pltpu.VMEM((HIDDEN,), BF16),
            pltpu.VMEM((HIDDEN,), BF16), pltpu.VMEM((HIDDEN + 2 * KV * HEAD_DIM,), BF16),
            pltpu.VMEM((ROWS, HIDDEN), F32), pltpu.VMEM((ROWS, HIDDEN), BF16),
            pltpu.VMEM((N_QKV, HIDDEN, QKV_CHUNK), BF16),
            pltpu.VMEM((N_PROJ, HIDDEN, PROJ_CHUNK), BF16),
            pltpu.VMEM((ROWS, FLAT, HEAD_DIM), BF16),
            pltpu.VMEM((ROWS, FLAT, HEAD_DIM), BF16),
            pltpu.VMEM((ROWS * HEADS, HEAD_DIM), F32),
            pltpu.VMEM((KV, ROWS, HEAD_DIM), F32),
            pltpu.VMEM((KV, ROWS, HEAD_DIM), F32),
            pltpu.VMEM((ROWS * HEADS, HEAD_DIM), F32),
            pltpu.VMEM((ROWS, HIDDEN), BF16),
            dma((5,)), dma((N_QKV,)), dma((N_PROJ,)), dma((N_SEQ,)), dma((N_SEQ,)), dma((N_SEQ,)), dma((N_SEQ,)), dma((2,)),
        ],
        compiler_params=pltpu.CompilerParams(vmem_limit_bytes=60 * 1024 * 1024),
        name="attn_block",
    )(lens, freq, x, ga, gm, bias, w_qkv, k_flat, v_flat, w_proj)


def mlp_kernel(m_hbm, h_hbm, win_hbm, wout_hbm, y_ref,
               m_ref, h_ref, rows_buf, win_buf, wout_buf, g_buf, pair_send, pair_recv, near_send, near_recv, far_keep, far_send, far_recv,
               own_acc, in_sem, win_sem, wout_sem, agx_s, agx_r, agp_s, agp_r, agr_s, agr_r,
               ps_s, ps_r, ns_s, ns_r, fs_s, fs_r):
    me = lax.axis_index('grp')
    partner = me + 1 - 2 * (me % 2)
    cross = (me + 2) % 4

    def win_copy(i, part, width):
        rows = pl.ds(i * F_CHUNK, width)
        return pltpu.make_async_copy(win_hbm.at[part, rows], win_buf.at[part, rows], win_sem.at[part, i])

    def wout_copy(j):
        cols = pl.ds(j * D_CHUNK, D_CHUNK)
        return pltpu.make_async_copy(wout_hbm.at[:, cols], wout_buf.at[:, cols], wout_sem.at[j])

    m_copy = pltpu.make_async_copy(m_hbm, m_ref, in_sem.at[0])
    h_copy = pltpu.make_async_copy(h_hbm, h_ref, in_sem.at[1])
    m_copy.start()
    tail = FFN_LOC - (N_F - 1) * F_CHUNK
    widths = [F_CHUNK] * (N_F - 1) + [tail]
    for i in range(N_F):
        for part in range(2):
            win_copy(i, part, widths[i]).start(priority=1)
    h_copy.start()

    barrier = pltpu.get_barrier_semaphore()
    for peer in (partner, cross):
        pl.semaphore_signal(barrier, inc=1, device_id={'grp': peer}, device_id_type=pl.DeviceIdType.MESH)
    pl.semaphore_wait(barrier, 2)

    def send(src, dst, ssem, rsem, peer):
        return pltpu.make_async_remote_copy(src_ref=src, dst_ref=dst, send_sem=ssem, recv_sem=rsem,
                                            device_id={'grp': peer}, device_id_type=pl.DeviceIdType.MESH)

    cross_copies = [send(m_ref.at[pl.ds(p * AG_ROWS, AG_ROWS)], rows_buf.at[pl.ds(2 * ROWS + p * AG_ROWS, AG_ROWS)],
                         agx_s.at[p], agx_r.at[p], cross) for p in range(AG_PIECES)]
    m_copy.wait()
    for cp in cross_copies:
        cp.start()
    pair_copy = send(m_ref, rows_buf.at[pl.ds(ROWS, ROWS)], agp_s, agp_r, partner)
    pair_copy.start()
    rows_buf[pl.ds(0, ROWS), :] = m_ref[...]
    relays = []
    for p in range(AG_PIECES):
        cross_copies[p].wait_recv()
        relay = send(rows_buf.at[pl.ds(2 * ROWS + p * AG_ROWS, AG_ROWS)],
                     rows_buf.at[pl.ds(3 * ROWS + p * AG_ROWS, AG_ROWS)], agr_s.at[p], agr_r.at[p], partner)
        relay.start()
        relays.append(relay)
    pair_copy.wait()
    for p in range(AG_PIECES):
        cross_copies[p].wait_send()
        relays[p].wait()

    def ffn_chunk(i, width):
        fr = pl.ds(i * F_CHUNK, width)
        rows = rows_buf[...]
        dims = (((1,), (1,)), ((), ()))
        gate = lax.dot_general(rows, win_buf[0, fr, :], dims, preferred_element_type=F32)
        up = lax.dot_general(rows, win_buf[1, fr, :], dims, preferred_element_type=F32)
        g_buf[:, fr] = (gate * jax.nn.sigmoid(gate) * up).astype(BF16)

    for j in range(N_D):
        wout_copy(j).start(priority=1)
    for i in range(N_F):
        for part in range(2):
            win_copy(i, part, widths[i]).wait()
    for i in range(N_F):
        ffn_chunk(i, widths[i])
    for j in range(N_D):
        wout_copy(j).wait()
    h_copy.wait()

    pair_copies = [send(pair_send.at[j], pair_recv.at[j], ps_s.at[j], ps_r.at[j], partner) for j in range(N_D)]
    near_copies = [send(near_send.at[j], near_recv.at[j], ns_s.at[j], ns_r.at[j], partner) for j in range(N_D)]
    far_copies = [send(far_send.at[j], far_recv.at[j], fs_s.at[j], fs_r.at[j], cross) for j in range(N_D)]

    def remote_block(j):
        cols = slice(j * D_CHUNK, (j + 1) * D_CHUNK)
        part = jnp.dot(g_buf[2 * ROWS:, :], wout_buf[:, cols], preferred_element_type=F32)
        far_keep[j] = part[:ROWS]
        pair_send[j] = part[ROWS:].astype(BF16)

    def local_block(j):
        cols = slice(j * D_CHUNK, (j + 1) * D_CHUNK)
        part = jnp.dot(g_buf[:2 * ROWS, :], wout_buf[:, cols], preferred_element_type=F32)
        own_acc[j] = part[:ROWS] + h_ref[:, cols]
        near_send[j] = part[ROWS:].astype(BF16)

    def pair_sum(j):
        pair_copies[j].wait_recv()
        far_send[j] = (far_keep[j] + pair_recv[j].astype(F32)).astype(BF16)

    half = N_D // 2
    for j in range(half):
        remote_block(j)
    for j in range(half):
        pair_copies[j].start()
    for j in range(half, N_D):
        remote_block(j)
    for j in range(half, N_D):
        pair_copies[j].start()
    for j in range(half):
        pair_sum(j)
    local_block(0)
    local_block(1)
    for j in range(half):
        far_copies[j].start()
    for j in range(2, half):
        local_block(j)
    for j in range(half, N_D):
        pair_sum(j)
    for j in range(half, N_D):
        local_block(j)
        far_copies[j].start()
    for j in range(N_D):
        near_copies[j].start()

    for j in range(N_D):
        cols = slice(j * D_CHUNK, (j + 1) * D_CHUNK)
        near_copies[j].wait_recv()
        far_copies[j].wait_recv()
        y_ref[:, cols] = (own_acc[j] + near_recv[j].astype(F32) + far_recv[j].astype(F32)).astype(BF16)
    for j in range(N_D):
        pair_copies[j].wait_send()
        near_copies[j].wait_send()
        far_copies[j].wait_send()


def mlp(m, h, w_in, w_out):
    vmem = pl.BlockSpec(memory_space=pltpu.VMEM)
    hbm = pl.BlockSpec(memory_space=pl.ANY)
    dma = pltpu.SemaphoreType.DMA
    piece = (N_D, ROWS, D_CHUNK)
    return pl.pallas_call(
        mlp_kernel,
        out_shape=jax.ShapeDtypeStruct((ROWS, HIDDEN), BF16),
        in_specs=[hbm] * 4,
        out_specs=vmem,
        scratch_shapes=[
            pltpu.VMEM((ROWS, HIDDEN), BF16), pltpu.VMEM((ROWS, HIDDEN), F32),
            pltpu.VMEM((4 * ROWS, HIDDEN), BF16),
            pltpu.VMEM((2, FFN_LOC, HIDDEN), BF16),
            pltpu.VMEM((FFN_LOC, HIDDEN), BF16),
            pltpu.VMEM((4 * ROWS, FFN_LOC), BF16),
            pltpu.VMEM(piece, BF16), pltpu.VMEM(piece, BF16),
            pltpu.VMEM(piece, BF16), pltpu.VMEM(piece, BF16),
            pltpu.VMEM(piece, F32), pltpu.VMEM(piece, BF16), pltpu.VMEM(piece, BF16),
            pltpu.VMEM(piece, F32),
            dma((2,)), dma((2, N_F)), dma((N_D,)),
            dma((AG_PIECES,)), dma((AG_PIECES,)), dma, dma, dma((AG_PIECES,)), dma((AG_PIECES,)),
            dma((N_D,)), dma((N_D,)), dma((N_D,)), dma((N_D,)), dma((N_D,)), dma((N_D,)),
        ],
        compiler_params=pltpu.CompilerParams(vmem_limit_bytes=60 * 1024 * 1024, collective_id=0, has_side_effects=True),
        name="mlp_block",
    )(m, h, w_in, w_out)


def rope_freq():
    pair = 2 * (np.arange(HEAD_DIM) // 2)
    return jnp.asarray((ROPE_BASE ** (-pair / (HEAD_DIM // 2)))[None, :], F32)


def solution(mesh):
    row_spec = P(('rep', 'grp'))
    repl_spec = P()

    def local_layer(x_in, seq_len, k_cache, v_cache, gamma_attn, w_qkv, b_qkv, w_proj, gamma_mlp, w_in, w_out):
        k_flat = k_cache.reshape(ROWS, FLAT, HEAD_DIM)
        v_flat = v_cache.reshape(ROWS, FLAT, HEAD_DIM)
        h, m, k_out, v_out = attention(seq_len, rope_freq(), x_in, gamma_attn, gamma_mlp, b_qkv, w_qkv, k_flat, v_flat, w_proj)
        layer_out = mlp(m, h, w_in, w_out)
        return layer_out, k_out.reshape(k_cache.shape), v_out.reshape(v_cache.shape)

    return jax.shard_map(local_layer, mesh=mesh,
                         in_specs=(row_spec, row_spec, row_spec, row_spec, repl_spec, repl_spec, repl_spec,
                                   repl_spec, repl_spec, P(None, 'grp', None), P('grp', None)),
                         out_specs=(row_spec, row_spec, row_spec), check_vma=False)
```

time: 65.4 us -> 51.9 us (0.79)
  Pallas kernels: 57.5 us -> 49.5 us
  other arithmetic: 4.05 us -> 0 us
  local copies, waits for them, and re-layouts: 2.96 us -> 1.67 us
    pallas_call x1, Pallas kernels: 33.8 us -> 29.5 us  [mlp(): pl.pallas_call(mlp_kernel, out_shape=jax.ShapeDtypeStruct((ROWS, HIDDEN),...]
    pallas_call x1, Pallas kernels: 23.7 us -> 20 us  [attention(): pl.pallas_call(attn_kernel, out_shape=(jax.ShapeDtypeStruct((ROWS, HIDDEN...]
    broadcast_in_dim x2 -> x0, other arithmetic: 2.55 us -> none  [the longest x1 1.28 us: local_layer(): gm = gamma_mlp.astype(F32)[None, :]]
    broadcast_in_dim x1 -> x0, local copies, waits for them, and re-layouts: 1.29 us -> none  [local_layer(): bias = b_qkv.astype(F32)[None, :]]
    select_n x2 -> x0, other arithmetic: 0.84 us -> none  [the longest x1 0.83 us: rope_tables(): jnp.where(active, jnp.sin(angles) * sign, 0.0)]
    convert_element_type x1 -> x0, other arithmetic: 0.66 us -> none  [rope_tables(): angles = lens.astype(F32)[:, None] * inv_freq[None, :]]
where the time goes in v2:
time: 51.9 us; the launch traced here: 51.8 us
  Pallas kernels  49.5 us (95%)
  local copies, waits for them, and re-layouts  1.67 us (3%)
  between operations  0.65 us (1%)
    pallas_call x1, Pallas kernels, mlp(): pl.pallas_call(mlp_kernel, out_shape=jax.ShapeDtypeStruct((ROWS, HIDDEN),...  29.5 us
    pallas_call x1, Pallas kernels, attention(): pl.pallas_call(attn_kernel, out_shape=(jax.ShapeDtypeStruct((ROWS, HIDDEN...  20 us
    unnamed x1, local copies, waits for them, and re-layouts  1.67 us

profile of v2, /device:TPU:0, one launch (start us, length us, event | category | flops | bytes accessed | tf_op | source)
XLA Modules:
  0.0 51.8 jit_solution(6215797617739905963)
XLA Ops:
  0.6 20.0 %attn_block.1 = (f32[64,2048]{1,0:T(8,128)}, bf16[64,2048]{1,0:T(8,128)(2,1)}, bf16[64,512,128]{2,1,0:T(8,128)(2,1)}, bf16[64,512,128]{2,1,0:T(8,128)(2,1)}) custom-call(s32[64]{0:T(128)} %len_ref.1, f32[1,128]{1,0:T(1,128)} %constant.2.clone.freq_hbm, bf16[64,2048]{1,0:T(8,128)(2,1)} %x_hbm.1, bf16[2048]{0:T(1024)(128)(2,1)} %ga_hbm.1, ...), custom_call_target="tpu_custom_call" | custom-call | tf_op jit(solution)/shard_map/attn_block/pallas_call | solution.py:205
  20.6 29.5 %mlp_block.1 = bf16[64,2048]{1,0:T(8,128)(2,1)} custom-call(bf16[64,2048]{1,0:T(8,128)(2,1)} %get-tuple-element.7.m_hbm, f32[64,2048]{1,0:T(8,128)} %get-tuple-element.8.h_hbm, bf16[2,2752,2048]{2,1,0:T(8,128)(2,1)} %win_hbm.1, bf16[2752,2048]{1,0:T(8,128)(2,1)} %wout_hbm.1), custom_call_target="tpu_custom_call" | custom-call | tf_op jit(solution)/shard_map/mlp_block/pallas_call | solution.py:366
  50.1 1.7 %copy.16 = bf16[64,2048]{1,0:T(8,128)(2,1)} copy(bf16[64,2048]{1,0:T(8,128)(2,1)} %mlp_block.1) | data formatting | bytes 524288

commit v3 on v2

--- a/solution.py
+++ b/solution.py
@@ -22,15 +22,19 @@
 N_PROJ = 4
 SEQ_CHUNK = 8
 N_SEQ = ROWS // SEQ_CHUNK
-SUB = 8
 WINDOW = 7
+OUT_LAG = 3
 F_CHUNK = 256
 N_F = 11
-D_CHUNK = 256
-N_D = HIDDEN // D_CHUNK
+D_EDGES = (0, 512, 1024, 1536, 2048)
+N_D = len(D_EDGES) - 1
+PAIR_LAG = 2
 AG_PIECES = 4
 AG_ROWS = ROWS // AG_PIECES
-LAG = 6
+RING = 5
+N_W = 4
+W_ROWS = FFN_LOC // N_W
+RELAY_AT = (6, 8, 10)
 F32 = jnp.float32
 BF16 = jnp.bfloat16
 
@@ -39,7 +43,7 @@
                 h_hbm, m_hbm, kout_hbm, vout_hbm,
                 freq_ref, x_ref, ga_ref, gm_ref, b_ref, h_ref, m_ref,
                 wq_buf, wp_buf, k_buf, v_buf, q_scr, kn_scr, vn_scr, ctx_scr, act_buf,
-                small_sem, wq_sem, wp_sem, k_sem, v_sem, ko_sem, vo_sem, out_sem):
+                small_sem, wq_sem, wp_sem, k_sem, v_sem, out_sem):
     small = [pltpu.make_async_copy(src, dst, small_sem.at[n]) for n, (src, dst) in enumerate(
         ((x_hbm, x_ref), (ga_hbm, ga_ref), (freq_hbm, freq_ref), (b_hbm, b_ref), (gm_hbm, gm_ref)))]
 
@@ -59,11 +63,11 @@
 
     def ko_copy(i):
         rows = pl.ds(i * SEQ_CHUNK, SEQ_CHUNK)
-        return pltpu.make_async_copy(k_buf.at[rows], kout_hbm.at[rows], ko_sem.at[i])
+        return pltpu.make_async_copy(k_buf.at[rows], kout_hbm.at[rows], k_sem.at[i])
 
     def vo_copy(i):
         rows = pl.ds(i * SEQ_CHUNK, SEQ_CHUNK)
-        return pltpu.make_async_copy(v_buf.at[rows], vout_hbm.at[rows], vo_sem.at[i])
+        return pltpu.make_async_copy(v_buf.at[rows], vout_hbm.at[rows], v_sem.at[i])
 
     for cp in small:
         cp.start()
@@ -125,19 +129,7 @@
     head_row = lax.broadcasted_iota(jnp.int32, (HEADS, FLAT), 0)
     pos = jnp.where((col % KV) == (head_row // (HEADS // KV)), col // KV, 2 * LMAX)
 
-    def chunk_body(i, carry):
-        k_copy(i).wait()
-        v_copy(i).wait()
-
-        @pl.when(i + WINDOW < N_SEQ)
-        def _():
-            k_copy(i + WINDOW).start()
-            v_copy(i + WINDOW).start()
-
-        @pl.when(jnp.logical_and(i + WINDOW >= N_SEQ, i + WINDOW < N_SEQ + N_PROJ))
-        def _():
-            wp_copy(i + WINDOW - N_SEQ).start()
-
+    def insert(i):
         for u in range(SEQ_CHUNK):
             b = i * SEQ_CHUNK + u
             ln = len_ref[b]
@@ -147,33 +139,56 @@
                 fresh = jnp.where(row16 % 2 == 0, new[0, pl.ds(b, 1), :], new[1, pl.ds(b, 1), :])
                 old = buf[b, pl.ds(base, 16), :].astype(F32)
                 buf[b, pl.ds(base, 16), :] = jnp.where(hit, fresh, old).astype(BF16)
-        for s0 in range(0, SEQ_CHUNK, SUB):
-            probs = []
-            for u in range(s0, s0 + SUB, 2):
-                b = i * SEQ_CHUNK + u
-                q = q_scr[pl.ds(pl.multiple_of(b * HEADS, 2 * HEADS), 2 * HEADS), :]
-                first = row32 < HEADS
-                q2 = jnp.concatenate([jnp.where(first, q, 0.0), jnp.where(first, 0.0, q)], axis=1).astype(BF16)
-                k2 = jnp.concatenate([k_buf[b], k_buf[b + 1]], axis=1)
-                s2 = lax.dot_general(q2, k2, (((1,), (1,)), ((), ())), preferred_element_type=F32)
-                pair = []
-                for t in range(2):
-                    s = jnp.where(pos <= len_ref[b + t], s2[t * HEADS:(t + 1) * HEADS], -jnp.inf)
-                    e = jnp.exp((s - jnp.max(s, axis=1, keepdims=True)) * (HEAD_DIM ** -0.5))
-                    pair.append((e * (1.0 / jnp.sum(e, axis=1, keepdims=True))).astype(BF16))
-                probs.append(jnp.concatenate(pair, axis=0))
-            for u in range(s0, s0 + SUB, 2):
-                b = i * SEQ_CHUNK + u
-                v2 = jnp.concatenate([v_buf[b], v_buf[b + 1]], axis=1)
-                c2 = jnp.dot(probs[(u - s0) // 2], v2, preferred_element_type=F32)
-                at = pl.multiple_of(b * HEADS, 2 * HEADS)
-                ctx_scr[pl.ds(at, HEADS), :] = c2[:HEADS, :HEAD_DIM]
-                ctx_scr[pl.ds(at + HEADS, HEADS), :] = c2[HEADS:, HEAD_DIM:]
+
+    def scores(i):
+        out = []
+        for u in range(0, SEQ_CHUNK, 2):
+            b = i * SEQ_CHUNK + u
+            q = q_scr[pl.ds(b * HEADS, 2 * HEADS), :]
+            first = row32 < HEADS
+            q2 = jnp.concatenate([jnp.where(first, q, 0.0), jnp.where(first, 0.0, q)], axis=1).astype(BF16)
+            k2 = jnp.concatenate([k_buf[b], k_buf[b + 1]], axis=1)
+            out.append(lax.dot_general(q2, k2, (((1,), (1,)), ((), ())), preferred_element_type=F32))
+        return out
+
+    def probabilities(i, raw):
+        probs = []
+        for u in range(0, SEQ_CHUNK, 2):
+            b = i * SEQ_CHUNK + u
+            s2 = raw[u // 2]
+            pair = []
+            for t in range(2):
+                s = jnp.where(pos <= len_ref[b + t], s2[t * HEADS:(t + 1) * HEADS], -jnp.inf)
+                e = jnp.exp((s - jnp.max(s, axis=1, keepdims=True)) * (HEAD_DIM ** -0.5))
+                pair.append((e * (1.0 / jnp.sum(e, axis=1, keepdims=True))).astype(BF16))
+            probs.append(jnp.concatenate(pair, axis=0))
+        return probs
+
+    def weighted_values(i, probs):
+        for u in range(0, SEQ_CHUNK, 2):
+            b = i * SEQ_CHUNK + u
+            v2 = jnp.concatenate([v_buf[b], v_buf[b + 1]], axis=1)
+            c2 = jnp.dot(probs[u // 2], v2, preferred_element_type=F32)
+            ctx_scr[pl.ds(b * HEADS, HEADS), :] = c2[:HEADS, :HEAD_DIM]
+            ctx_scr[pl.ds((b + 1) * HEADS, HEADS), :] = c2[HEADS:, HEAD_DIM:]
+
+    probs = None
+    for i in range(N_SEQ):
+        k_copy(i).wait()
+        v_copy(i).wait()
+        fetch(N_QKV + i + WINDOW)
+        if i >= OUT_LAG:
+            ko_copy(i - OUT_LAG).start()
+            vo_copy(i - OUT_LAG).start()
+        insert(i)
+        raw = scores(i)
+        if i > 0:
+            weighted_values(i - 1, probs)
+        probs = probabilities(i, raw)
+    for i in range(N_SEQ - OUT_LAG, N_SEQ):
         ko_copy(i).start()
         vo_copy(i).start()
-        return carry
-
-    lax.fori_loop(0, N_SEQ, chunk_body, 0)
+    weighted_values(N_SEQ - 1, probs)
 
     for h in range(HEADS):
         act_buf[:, h * HEAD_DIM:(h + 1) * HEAD_DIM] = ctx_scr[pl.ds(h, ROWS, stride=HEADS), :].astype(BF16)
@@ -221,7 +236,7 @@
             pltpu.VMEM((KV, ROWS, HEAD_DIM), F32),
             pltpu.VMEM((ROWS * HEADS, HEAD_DIM), F32),
             pltpu.VMEM((ROWS, HIDDEN), BF16),
-            dma((5,)), dma((N_QKV,)), dma((N_PROJ,)), dma((N_SEQ,)), dma((N_SEQ,)), dma((N_SEQ,)), dma((N_SEQ,)), dma((2,)),
+            dma((5,)), dma((N_QKV,)), dma((N_PROJ,)), dma((N_SEQ,)), dma((N_SEQ,)), dma((2,)),
         ],
         compiler_params=pltpu.CompilerParams(vmem_limit_bytes=60 * 1024 * 1024),
         name="attn_block",
@@ -229,29 +244,28 @@
 
 
 def mlp_kernel(m_hbm, h_hbm, win_hbm, wout_hbm, y_ref,
-               m_ref, h_ref, rows_buf, win_buf, wout_buf, g_buf, pair_send, pair_recv, near_send, near_recv, far_keep, far_send, far_recv,
+               m_ref, h_ref, rows_buf, win_buf, wint_buf, wout_buf, g_buf, pair_send, pair_recv, near_send, near_recv, far_keep, far_send, far_recv,
                own_acc, in_sem, win_sem, wout_sem, agx_s, agx_r, agp_s, agp_r, agr_s, agr_r,
                ps_s, ps_r, ns_s, ns_r, fs_s, fs_r):
     me = lax.axis_index('grp')
     partner = me + 1 - 2 * (me % 2)
     cross = (me + 2) % 4
 
-    def win_copy(i, part, width):
-        rows = pl.ds(i * F_CHUNK, width)
-        return pltpu.make_async_copy(win_hbm.at[part, rows], win_buf.at[part, rows], win_sem.at[part, i])
+    def win_copy(i, width):
+        src = win_hbm.at[:, pl.ds(i * F_CHUNK, width)]
+        return pltpu.make_async_copy(src, win_buf.at[i % RING, :, pl.ds(0, width)], win_sem.at[i % RING])
 
     def wout_copy(j):
-        cols = pl.ds(j * D_CHUNK, D_CHUNK)
-        return pltpu.make_async_copy(wout_hbm.at[:, cols], wout_buf.at[:, cols], wout_sem.at[j])
+        rows = pl.ds(j * W_ROWS, W_ROWS)
+        return pltpu.make_async_copy(wout_hbm.at[rows], wout_buf.at[rows], wout_sem.at[j])
 
     m_copy = pltpu.make_async_copy(m_hbm, m_ref, in_sem.at[0])
     h_copy = pltpu.make_async_copy(h_hbm, h_ref, in_sem.at[1])
     m_copy.start()
     tail = FFN_LOC - (N_F - 1) * F_CHUNK
     widths = [F_CHUNK] * (N_F - 1) + [tail]
-    for i in range(N_F):
-        for part in range(2):
-            win_copy(i, part, widths[i]).start(priority=1)
+    for i in range(RING):
+        win_copy(i, widths[i]).start(priority=1)
     h_copy.start()
 
     barrier = pltpu.get_barrier_semaphore()
@@ -271,98 +285,93 @@
     pair_copy = send(m_ref, rows_buf.at[pl.ds(ROWS, ROWS)], agp_s, agp_r, partner)
     pair_copy.start()
     rows_buf[pl.ds(0, ROWS), :] = m_ref[...]
-    relays = []
-    for p in range(AG_PIECES):
+    relays = [send(rows_buf.at[pl.ds(2 * ROWS + p * AG_ROWS, AG_ROWS)],
+                   rows_buf.at[pl.ds(3 * ROWS + p * AG_ROWS, AG_ROWS)], agr_s.at[p], agr_r.at[p], partner)
+              for p in range(AG_PIECES)]
+
+    def swiglu(rows, i, width, top, weights):
+        gate = jnp.dot(rows, weights[0], preferred_element_type=F32)
+        up = jnp.dot(rows, weights[1], preferred_element_type=F32)
+        g_buf[pl.ds(top, 2 * ROWS), pl.ds(i * F_CHUNK, width)] = (gate * jax.nn.sigmoid(gate) * up).astype(BF16)
+
+    for i in range(N_F):
+        win_copy(i, widths[i]).wait()
+        for part in range(2):
+            wint_buf[i, part, :, :widths[i]] = win_buf[i % RING, part, :widths[i], :].T
+        if i + RING < N_F:
+            win_copy(i + RING, widths[i + RING]).start(priority=1)
+        if i == 1:
+            pair_copy.wait()
+        if i >= 1:
+            swiglu(rows_buf[pl.ds(0, 2 * ROWS), :], i - 1, F_CHUNK, 0, [wint_buf[i - 1, part] for part in range(2)])
+        if i in RELAY_AT:
+            p = RELAY_AT.index(i)
+            cross_copies[p].wait_recv()
+            relays[p].start()
+    swiglu(rows_buf[pl.ds(0, 2 * ROWS), :], N_F - 1, tail, 0, [wint_buf[N_F - 1, part, :, :tail] for part in range(2)])
+    for j in range(N_W):
+        wout_copy(j).start(priority=1)
+    for p in range(len(RELAY_AT), AG_PIECES):
         cross_copies[p].wait_recv()
-        relay = send(rows_buf.at[pl.ds(2 * ROWS + p * AG_ROWS, AG_ROWS)],
-                     rows_buf.at[pl.ds(3 * ROWS + p * AG_ROWS, AG_ROWS)], agr_s.at[p], agr_r.at[p], partner)
-        relay.start()
-        relays.append(relay)
-    pair_copy.wait()
+        relays[p].start()
     for p in range(AG_PIECES):
         cross_copies[p].wait_send()
         relays[p].wait()
-
-    def ffn_chunk(i, width):
-        fr = pl.ds(i * F_CHUNK, width)
-        rows = rows_buf[...]
-        dims = (((1,), (1,)), ((), ()))
-        gate = lax.dot_general(rows, win_buf[0, fr, :], dims, preferred_element_type=F32)
-        up = lax.dot_general(rows, win_buf[1, fr, :], dims, preferred_element_type=F32)
-        g_buf[:, fr] = (gate * jax.nn.sigmoid(gate) * up).astype(BF16)
-
-    for j in range(N_D):
-        wout_copy(j).start(priority=1)
     for i in range(N_F):
-        for part in range(2):
-            win_copy(i, part, widths[i]).wait()
-    for i in range(N_F):
-        ffn_chunk(i, widths[i])
-    for j in range(N_D):
+        swiglu(rows_buf[pl.ds(2 * ROWS, 2 * ROWS), :], i, widths[i], 2 * ROWS,
+               [wint_buf[i, part, :, :widths[i]] for part in range(2)])
+    for j in range(N_W):
         wout_copy(j).wait()
     h_copy.wait()
 
-    pair_copies = [send(pair_send.at[j], pair_recv.at[j], ps_s.at[j], ps_r.at[j], partner) for j in range(N_D)]
-    near_copies = [send(near_send.at[j], near_recv.at[j], ns_s.at[j], ns_r.at[j], partner) for j in range(N_D)]
-    far_copies = [send(far_send.at[j], far_recv.at[j], fs_s.at[j], fs_r.at[j], cross) for j in range(N_D)]
-
-    def remote_block(j):
-        cols = slice(j * D_CHUNK, (j + 1) * D_CHUNK)
-        part = jnp.dot(g_buf[2 * ROWS:, :], wout_buf[:, cols], preferred_element_type=F32)
-        far_keep[j] = part[:ROWS]
-        pair_send[j] = part[ROWS:].astype(BF16)
-
-    def local_block(j):
-        cols = slice(j * D_CHUNK, (j + 1) * D_CHUNK)
-        part = jnp.dot(g_buf[:2 * ROWS, :], wout_buf[:, cols], preferred_element_type=F32)
-        own_acc[j] = part[:ROWS] + h_ref[:, cols]
-        near_send[j] = part[ROWS:].astype(BF16)
-
-    def pair_sum(j):
-        pair_copies[j].wait_recv()
-        far_send[j] = (far_keep[j] + pair_recv[j].astype(F32)).astype(BF16)
-
-    half = N_D // 2
-    for j in range(half):
-        remote_block(j)
-    for j in range(half):
-        pair_copies[j].start()
-    for j in range(half, N_D):
-        remote_block(j)
-    for j in range(half, N_D):
-        pair_copies[j].start()
-    for j in range(half):
-        pair_sum(j)
-    local_block(0)
-    local_block(1)
-    for j in range(half):
-        far_copies[j].start()
-    for j in range(2, half):
-        local_block(j)
-    for j in range(half, N_D):
-        pair_sum(j)
-    for j in range(half, N_D):
-        local_block(j)
-        far_copies[j].start()
-    for j in range(N_D):
-        near_copies[j].start()
-
-    for j in range(N_D):
-        cols = slice(j * D_CHUNK, (j + 1) * D_CHUNK)
-        near_copies[j].wait_recv()
-        far_copies[j].wait_recv()
-        y_ref[:, cols] = (own_acc[j] + near_recv[j].astype(F32) + far_recv[j].astype(F32)).astype(BF16)
-    for j in range(N_D):
-        pair_copies[j].wait_send()
-        near_copies[j].wait_send()
-        far_copies[j].wait_send()
+    def piece(k):
+        return pl.ds(D_EDGES[k], D_EDGES[k + 1] - D_EDGES[k])
+
+    def block_send(src, dst, ssem, rsem, peer):
+        return [send(src.at[:, piece(k)], dst.at[:, piece(k)], ssem.at[k], rsem.at[k], peer) for k in range(N_D)]
+
+    pair_copies = block_send(pair_send, pair_recv, ps_s, ps_r, partner)
+    near_copies = block_send(near_send, near_recv, ns_s, ns_r, partner)
+    far_copies = block_send(far_send, far_recv, fs_s, fs_r, cross)
+
+    def remote_block(k):
+        part = jnp.dot(g_buf[2 * ROWS:, :], wout_buf[:, piece(k)], preferred_element_type=F32)
+        far_keep[:, piece(k)] = part[:ROWS]
+        pair_send[:, piece(k)] = part[ROWS:].astype(BF16)
+        pair_copies[k].start()
+
+    def local_block(k):
+        part = jnp.dot(g_buf[:2 * ROWS, :], wout_buf[:, piece(k)], preferred_element_type=F32)
+        own_acc[:, piece(k)] = part[:ROWS] + h_ref[:, piece(k)]
+        near_send[:, piece(k)] = part[ROWS:].astype(BF16)
+        near_copies[k].start()
+
+    def pair_sum(k):
+        pair_copies[k].wait_recv()
+        far_send[:, piece(k)] = (far_keep[:, piece(k)] + pair_recv[:, piece(k)].astype(F32)).astype(BF16)
+        far_copies[k].start()
+
+    steps = [(remote_block, k) for k in range(N_D)] + [(local_block, k) for k in range(N_D)]
+    for n, (step, k) in enumerate(steps):
+        step(k)
+        if 0 <= n - PAIR_LAG < N_D:
+            pair_sum(n - PAIR_LAG)
+    for k in range(N_D):
+        near_copies[k].wait_recv()
+        far_copies[k].wait_recv()
+        y_ref[:, piece(k)] = (own_acc[:, piece(k)] + near_recv[:, piece(k)].astype(F32)
+                              + far_recv[:, piece(k)].astype(F32)).astype(BF16)
+    for k in range(N_D):
+        pair_copies[k].wait_send()
+        near_copies[k].wait_send()
+        far_copies[k].wait_send()
 
 
 def mlp(m, h, w_in, w_out):
     vmem = pl.BlockSpec(memory_space=pltpu.VMEM)
     hbm = pl.BlockSpec(memory_space=pl.ANY)
     dma = pltpu.SemaphoreType.DMA
-    piece = (N_D, ROWS, D_CHUNK)
+    piece = (ROWS, HIDDEN)
     return pl.pallas_call(
         mlp_kernel,
         out_shape=jax.ShapeDtypeStruct((ROWS, HIDDEN), BF16),
@@ -371,14 +380,15 @@
         scratch_shapes=[
             pltpu.VMEM((ROWS, HIDDEN), BF16), pltpu.VMEM((ROWS, HIDDEN), F32),
             pltpu.VMEM((4 * ROWS, HIDDEN), BF16),
-            pltpu.VMEM((2, FFN_LOC, HIDDEN), BF16),
+            pltpu.VMEM((RING, 2, F_CHUNK, HIDDEN), BF16),
+            pltpu.VMEM((N_F, 2, HIDDEN, F_CHUNK), BF16),
             pltpu.VMEM((FFN_LOC, HIDDEN), BF16),
             pltpu.VMEM((4 * ROWS, FFN_LOC), BF16),
             pltpu.VMEM(piece, BF16), pltpu.VMEM(piece, BF16),
             pltpu.VMEM(piece, BF16), pltpu.VMEM(piece, BF16),
             pltpu.VMEM(piece, F32), pltpu.VMEM(piece, BF16), pltpu.VMEM(piece, BF16),
             pltpu.VMEM(piece, F32),
-            dma((2,)), dma((2, N_F)), dma((N_D,)),
+            dma((2,)), dma((RING,)), dma((N_W,)),
             dma((AG_PIECES,)), dma((AG_PIECES,)), dma, dma, dma((AG_PIECES,)), dma((AG_PIECES,)),
             dma((N_D,)), dma((N_D,)), dma((N_D,)), dma((N_D,)), dma((N_D,)), dma((N_D,)),
         ],

time: 51.9 us -> 47.3 us (0.911)
  Pallas kernels: 49.5 us -> 44.9 us
    pallas_call x1, Pallas kernels: 29.5 us -> 27.1 us  [mlp(): pl.pallas_call(mlp_kernel, out_shape=jax.ShapeDtypeStruct((ROWS, HIDDEN),...]
    pallas_call x1, Pallas kernels: 20 us -> 17.8 us  [attention(): pl.pallas_call(attn_kernel, out_shape=(jax.ShapeDtypeStruct((ROWS, HIDDEN...]
where the time goes in v3:
time: 47.3 us; the launch traced here: 47.2 us
  Pallas kernels  44.9 us (95%)
  local copies, waits for them, and re-layouts  1.67 us (4%)
  between operations  0.65 us (1%)
    pallas_call x1, Pallas kernels, mlp(): pl.pallas_call(mlp_kernel, out_shape=jax.ShapeDtypeStruct((ROWS, HIDDEN),...  27.1 us
    pallas_call x1, Pallas kernels, attention(): pl.pallas_call(attn_kernel, out_shape=(jax.ShapeDtypeStruct((ROWS, HIDDEN...  17.8 us
    unnamed x1, local copies, waits for them, and re-layouts  1.67 us

profile of v3, /device:TPU:0, one launch (start us, length us, event | category | flops | bytes accessed | tf_op | source)
XLA Modules:
  0.0 47.2 jit_solution(11628154209269314357)
XLA Ops:
  0.6 17.8 %attn_block.1 = (f32[64,2048]{1,0:T(8,128)}, bf16[64,2048]{1,0:T(8,128)(2,1)}, bf16[64,512,128]{2,1,0:T(8,128)(2,1)}, bf16[64,512,128]{2,1,0:T(8,128)(2,1)}) custom-call(s32[64]{0:T(128)} %len_ref.1, f32[1,128]{1,0:T(1,128)} %constant.2.clone.freq_hbm, bf16[64,2048]{1,0:T(8,128)(2,1)} %x_hbm.1, bf16[2048]{0:T(1024)(128)(2,1)} %ga_hbm.1, ...), custom_call_target="tpu_custom_call" | custom-call | tf_op jit(solution)/shard_map/attn_block/pallas_call | solution.py:220
  18.4 27.1 %mlp_block.1 = bf16[64,2048]{1,0:T(8,128)(2,1)} custom-call(bf16[64,2048]{1,0:T(8,128)(2,1)} %get-tuple-element.7.m_hbm, f32[64,2048]{1,0:T(8,128)} %get-tuple-element.8.h_hbm, bf16[2,2752,2048]{2,1,0:T(8,128)(2,1)} %win_hbm.1, bf16[2752,2048]{1,0:T(8,128)(2,1)} %wout_hbm.1), custom_call_target="tpu_custom_call" | custom-call | tf_op jit(solution)/shard_map/mlp_block/pallas_call | solution.py:375
  45.5 1.7 %copy.16 = bf16[64,2048]{1,0:T(8,128)(2,1)} copy(bf16[64,2048]{1,0:T(8,128)(2,1)} %mlp_block.1) | data formatting | bytes 524288

commit v4 on v3

--- a/solution.py
+++ b/solution.py
@@ -23,18 +23,22 @@
 SEQ_CHUNK = 8
 N_SEQ = ROWS // SEQ_CHUNK
 WINDOW = 7
-OUT_LAG = 3
+OUT_LAG = 4
 F_CHUNK = 256
 N_F = 11
 D_EDGES = (0, 512, 1024, 1536, 2048)
 N_D = len(D_EDGES) - 1
 PAIR_LAG = 2
 AG_PIECES = 4
-AG_ROWS = ROWS // AG_PIECES
-RING = 5
+AG_COLS = HIDDEN // AG_PIECES
+K_PARTS = ((0, HIDDEN // 2), (HIDDEN // 2, HIDDEN // 2))
+RING = 4
+CUT = 6
+N_T = 9
 N_W = 4
 W_ROWS = FFN_LOC // N_W
-RELAY_AT = (6, 8, 10)
+RELAY_AT = (5, 7)
+HBM_ROWS = 2048
 F32 = jnp.float32
 BF16 = jnp.bfloat16
 
@@ -202,8 +206,8 @@
         total = total + jnp.sum(hid * hid, axis=-1, keepdims=True)
     inv2 = lax.rsqrt(total * (1.0 / HIDDEN) + EPS)
     m_ref[...] = (h_ref[...] * inv2 * gm_ref[...].astype(F32).reshape(1, HIDDEN)).astype(BF16)
-    h_copy = pltpu.make_async_copy(h_ref, h_hbm, out_sem.at[0])
-    m_copy = pltpu.make_async_copy(m_ref, m_hbm, out_sem.at[1])
+    h_copy = pltpu.make_async_copy(h_ref, h_hbm.at[pl.ds(0, ROWS)], out_sem.at[0])
+    m_copy = pltpu.make_async_copy(m_ref, m_hbm.at[pl.ds(0, ROWS)], out_sem.at[1])
     h_copy.start()
     m_copy.start()
     for i in range(N_SEQ):
@@ -219,7 +223,7 @@
     dma = pltpu.SemaphoreType.DMA
     return pl.pallas_call(
         attn_kernel,
-        out_shape=(jax.ShapeDtypeStruct((ROWS, HIDDEN), F32), jax.ShapeDtypeStruct((ROWS, HIDDEN), BF16),
+        out_shape=(jax.ShapeDtypeStruct((HBM_ROWS, HIDDEN), F32), jax.ShapeDtypeStruct((HBM_ROWS, HIDDEN), BF16),
                    jax.ShapeDtypeStruct(k_flat.shape, BF16), jax.ShapeDtypeStruct(v_flat.shape, BF16)),
         in_specs=[smem] + [hbm] * 9,
         out_specs=(hbm,) * 4,
@@ -244,7 +248,7 @@
 
 
 def mlp_kernel(m_hbm, h_hbm, win_hbm, wout_hbm, y_ref,
-               m_ref, h_ref, rows_buf, win_buf, wint_buf, wout_buf, g_buf, pair_send, pair_recv, near_send, near_recv, far_keep, far_send, far_recv,
+               m_ref, h_ref, rows_buf, part_acc, late_acc, win_buf, wint_buf, wout_buf, g_buf, pair_send, pair_recv, near_send, near_recv, far_keep, far_send, far_recv,
                own_acc, in_sem, win_sem, wout_sem, agx_s, agx_r, agp_s, agp_r, agr_s, agr_r,
                ps_s, ps_r, ns_s, ns_r, fs_s, fs_r):
     me = lax.axis_index('grp')
@@ -259,8 +263,8 @@
         rows = pl.ds(j * W_ROWS, W_ROWS)
         return pltpu.make_async_copy(wout_hbm.at[rows], wout_buf.at[rows], wout_sem.at[j])
 
-    m_copy = pltpu.make_async_copy(m_hbm, m_ref, in_sem.at[0])
-    h_copy = pltpu.make_async_copy(h_hbm, h_ref, in_sem.at[1])
+    m_copy = pltpu.make_async_copy(m_hbm.at[pl.ds(0, ROWS)], m_ref, in_sem.at[0])
+    h_copy = pltpu.make_async_copy(h_hbm.at[pl.ds(0, ROWS)], h_ref, in_sem.at[1])
     m_copy.start()
     tail = FFN_LOC - (N_F - 1) * F_CHUNK
     widths = [F_CHUNK] * (N_F - 1) + [tail]
@@ -277,49 +281,96 @@
         return pltpu.make_async_remote_copy(src_ref=src, dst_ref=dst, send_sem=ssem, recv_sem=rsem,
                                             device_id={'grp': peer}, device_id_type=pl.DeviceIdType.MESH)
 
-    cross_copies = [send(m_ref.at[pl.ds(p * AG_ROWS, AG_ROWS)], rows_buf.at[pl.ds(2 * ROWS + p * AG_ROWS, AG_ROWS)],
-                         agx_s.at[p], agx_r.at[p], cross) for p in range(AG_PIECES)]
+    def part_of(slot, p):
+        return rows_buf.at[pl.ds(slot * ROWS, ROWS), pl.ds(p * AG_COLS, AG_COLS)]
+
+    cross_copies = [send(m_ref.at[:, pl.ds(p * AG_COLS, AG_COLS)], part_of(2, p), agx_s.at[p], agx_r.at[p], cross)
+                    for p in range(AG_PIECES)]
     m_copy.wait()
     for cp in cross_copies:
         cp.start()
     pair_copy = send(m_ref, rows_buf.at[pl.ds(ROWS, ROWS)], agp_s, agp_r, partner)
     pair_copy.start()
     rows_buf[pl.ds(0, ROWS), :] = m_ref[...]
-    relays = [send(rows_buf.at[pl.ds(2 * ROWS + p * AG_ROWS, AG_ROWS)],
-                   rows_buf.at[pl.ds(3 * ROWS + p * AG_ROWS, AG_ROWS)], agr_s.at[p], agr_r.at[p], partner)
-              for p in range(AG_PIECES)]
-
-    def swiglu(rows, i, width, top, weights):
-        gate = jnp.dot(rows, weights[0], preferred_element_type=F32)
-        up = jnp.dot(rows, weights[1], preferred_element_type=F32)
-        g_buf[pl.ds(top, 2 * ROWS), pl.ds(i * F_CHUNK, width)] = (gate * jax.nn.sigmoid(gate) * up).astype(BF16)
-
-    for i in range(N_F):
+    relays = [send(part_of(2, p), part_of(3, p), agr_s.at[p], agr_r.at[p], partner) for p in range(AG_PIECES)]
+
+    def gated(gate, up):
+        return (gate * jax.nn.sigmoid(gate) * up).astype(BF16)
+
+    def local_ffn(i):
+        rows = rows_buf[pl.ds(0, 2 * ROWS), :]
+        gate, up = [jnp.dot(rows, wint_buf[i, part, :, :widths[i]], preferred_element_type=F32) for part in range(2)]
+        g_buf[pl.ds(0, 2 * ROWS), pl.ds(i * F_CHUNK, widths[i])] = gated(gate, up)
+
+    def ahead_chunk(i, phase):
+        k0, size = K_PARTS[phase]
+        rows = rows_buf[pl.ds(2 * ROWS, 2 * ROWS), k0:k0 + size]
+        cols = pl.ds(i * F_CHUNK, widths[i])
+        sums = []
+        for part in range(2):
+            prod = jnp.dot(rows, wint_buf[i, part, k0:k0 + size, :], preferred_element_type=F32)
+            sums.append(prod if phase == 0 else part_acc[part, :, cols] + prod)
+        if phase < len(K_PARTS) - 1:
+            for part in range(2):
+                part_acc[part, :, cols] = sums[part]
+        else:
+            g_buf[pl.ds(2 * ROWS, 2 * ROWS), cols] = gated(sums[0], sums[1])
+
+    def late_chunk(i, phase):
+        k0, size = K_PARTS[phase]
+        rows = rows_buf[:, k0:k0 + size]
+        cols = pl.ds((i - N_T) * F_CHUNK, widths[i])
+        sums = []
+        for part in range(2):
+            prod = lax.dot_general(rows, win_buf[i % RING, part, :widths[i], k0:k0 + size],
+                                   (((1,), (1,)), ((), ())), preferred_element_type=F32)
+            sums.append(prod if phase == 0 else late_acc[part, :, cols] + prod)
+        if phase < len(K_PARTS) - 1:
+            for part in range(2):
+                late_acc[part, :, cols] = sums[part]
+        else:
+            g_buf[:, pl.ds(i * F_CHUNK, widths[i])] = gated(sums[0], sums[1])
+
+    def remote_phase(phase, first, last):
+        for i in range(first, last):
+            (ahead_chunk if i < N_T else late_chunk)(i, phase)
+
+    def relay(p):
+        cross_copies[p].wait_recv()
+        relays[p].start()
+
+    for i in range(N_T):
+        if i == 1:
+            pair_copy.wait()
         win_copy(i, widths[i]).wait()
         for part in range(2):
-            wint_buf[i, part, :, :widths[i]] = win_buf[i % RING, part, :widths[i], :].T
+            wint_buf[i, part] = win_buf[i % RING, part].T
         if i + RING < N_F:
             win_copy(i + RING, widths[i + RING]).start(priority=1)
-        if i == 1:
-            pair_copy.wait()
+        else:
+            wout_copy(i + RING - N_F).start(priority=1)
         if i >= 1:
-            swiglu(rows_buf[pl.ds(0, 2 * ROWS), :], i - 1, F_CHUNK, 0, [wint_buf[i - 1, part] for part in range(2)])
+            local_ffn(i - 1)
         if i in RELAY_AT:
-            p = RELAY_AT.index(i)
-            cross_copies[p].wait_recv()
-            relays[p].start()
-    swiglu(rows_buf[pl.ds(0, 2 * ROWS), :], N_F - 1, tail, 0, [wint_buf[N_F - 1, part, :, :tail] for part in range(2)])
-    for j in range(N_W):
+            relay(RELAY_AT.index(i))
+    for j in range(N_T + RING - N_F, N_W):
         wout_copy(j).start(priority=1)
-    for p in range(len(RELAY_AT), AG_PIECES):
-        cross_copies[p].wait_recv()
-        relays[p].start()
+    local_ffn(N_T - 1)
+    for i in range(N_T, N_F):
+        win_copy(i, widths[i]).wait()
+    if len(RELAY_AT) < 3:
+        relay(2)
+    for p in range(2):
+        relays[p].wait_recv()
+    remote_phase(0, 0, CUT)
+    relay(3)
+    remote_phase(0, CUT, N_F)
+    relays[2].wait_recv()
+    relays[3].wait_recv()
+    remote_phase(1, 0, N_F)
     for p in range(AG_PIECES):
         cross_copies[p].wait_send()
-        relays[p].wait()
-    for i in range(N_F):
-        swiglu(rows_buf[pl.ds(2 * ROWS, 2 * ROWS), :], i, widths[i], 2 * ROWS,
-               [wint_buf[i, part, :, :widths[i]] for part in range(2)])
+        relays[p].wait_send()
     for j in range(N_W):
         wout_copy(j).wait()
     h_copy.wait()
@@ -380,8 +431,10 @@
         scratch_shapes=[
             pltpu.VMEM((ROWS, HIDDEN), BF16), pltpu.VMEM((ROWS, HIDDEN), F32),
             pltpu.VMEM((4 * ROWS, HIDDEN), BF16),
+            pltpu.VMEM((2, 2 * ROWS, N_T * F_CHUNK), F32),
+            pltpu.VMEM((2, 4 * ROWS, (N_F - N_T) * F_CHUNK), F32),
             pltpu.VMEM((RING, 2, F_CHUNK, HIDDEN), BF16),
-            pltpu.VMEM((N_F, 2, HIDDEN, F_CHUNK), BF16),
+            pltpu.VMEM((N_T, 2, HIDDEN, F_CHUNK), BF16),
             pltpu.VMEM((FFN_LOC, HIDDEN), BF16),
             pltpu.VMEM((4 * ROWS, FFN_LOC), BF16),
             pltpu.VMEM(piece, BF16), pltpu.VMEM(piece, BF16),
@@ -392,7 +445,7 @@
             dma((AG_PIECES,)), dma((AG_PIECES,)), dma, dma, dma((AG_PIECES,)), dma((AG_PIECES,)),
             dma((N_D,)), dma((N_D,)), dma((N_D,)), dma((N_D,)), dma((N_D,)), dma((N_D,)),
         ],
-        compiler_params=pltpu.CompilerParams(vmem_limit_bytes=60 * 1024 * 1024, collective_id=0, has_side_effects=True),
+        compiler_params=pltpu.CompilerParams(vmem_limit_bytes=50 * 1024 * 1024, collective_id=0, has_side_effects=True),
         name="mlp_block",
     )(m, h, w_in, w_out)
 

time: 47.3 us -> 43.5 us (0.920)
  Pallas kernels: 44.9 us -> 42.1 us
  local copies, waits for them, and re-layouts: 1.67 us -> 0.71 us
    pallas_call x1, Pallas kernels: 27.1 us -> 24.7 us  [mlp(): pl.pallas_call(mlp_kernel, out_shape=jax.ShapeDtypeStruct((ROWS, HIDDEN),...]
    unnamed x1, local copies, waits for them, and re-layouts: 1.67 us -> 0.71 us
where the time goes in v4:
time: 43.5 us; the launch traced here: 43.4 us
  Pallas kernels  42.1 us (97%)
  local copies, waits for them, and re-layouts  0.71 us (2%)
  between operations  0.65 us (1%)
    pallas_call x1, Pallas kernels, mlp(): pl.pallas_call(mlp_kernel, out_shape=jax.ShapeDtypeStruct((ROWS, HIDDEN),...  24.7 us
    pallas_call x1, Pallas kernels, attention(): pl.pallas_call(attn_kernel, out_shape=(jax.ShapeDtypeStruct((HBM_ROWS, HI...  17.3 us

profile of v4, /device:TPU:0, one launch (start us, length us, event | category | flops | bytes accessed | tf_op | source)
XLA Modules:
  0.0 43.4 jit_solution(16002199669912351807)
XLA Ops:
  0.6 17.3 %attn_block.1 = (f32[2048,2048]{1,0:T(8,128)}, bf16[2048,2048]{1,0:T(8,128)(2,1)}, bf16[64,512,128]{2,1,0:T(8,128)(2,1)}, bf16[64,512,128]{2,1,0:T(8,128)(2,1)}) custom-call(s32[64]{0:T(128)} %len_ref.1, f32[1,128]{1,0:T(1,128)} %constant.2.clone.freq_hbm, bf16[64,2048]{1,0:T(8,128)(2,1)} %x_hbm.1, bf16[2048]{0:T(1024)(128)(2,1)} %ga_hbm.1, ...), custom_call_target="tpu_custom_call" | custom-call | tf_op jit(solution)/shard_map/attn_block/pallas_call | solution.py:224
  18.0 24.7 %mlp_block.1 = bf16[64,2048]{1,0:T(8,128)(2,1)S(1)} custom-call(bf16[2048,2048]{1,0:T(8,128)(2,1)} %get-tuple-element.7.m_hbm, f32[2048,2048]{1,0:T(8,128)} %get-tuple-element.8.h_hbm, bf16[2,2752,2048]{2,1,0:T(8,128)(2,1)} %win_hbm.1, bf16[2752,2048]{1,0:T(8,128)(2,1)} %wout_hbm.1), custom_call_target="tpu_custom_call" | custom-call | tf_op jit(solution)/shard_map/mlp_block/pallas_call | solution.py:426
  42.7 0.7 %copy.16 = bf16[64,2048]{1,0:T(8,128)(2,1)} copy(bf16[64,2048]{1,0:T(8,128)(2,1)S(1)} %mlp_block.1) | data formatting | bytes 524288

commit v5 on v4

--- a/solution.py
+++ b/solution.py
@@ -26,6 +26,7 @@
 OUT_LAG = 4
 F_CHUNK = 256
 N_F = 11
+DIRECT = 256
 D_EDGES = (0, 512, 1024, 1536, 2048)
 N_D = len(D_EDGES) - 1
 PAIR_LAG = 2
@@ -249,11 +250,12 @@
 
 def mlp_kernel(m_hbm, h_hbm, win_hbm, wout_hbm, y_ref,
                m_ref, h_ref, rows_buf, part_acc, late_acc, win_buf, wint_buf, wout_buf, g_buf, pair_send, pair_recv, near_send, near_recv, far_keep, far_send, far_recv,
-               own_acc, in_sem, win_sem, wout_sem, agx_s, agx_r, agp_s, agp_r, agr_s, agr_r,
-               ps_s, ps_r, ns_s, ns_r, fs_s, fs_r):
+               own_acc, direct_send, direct_recv, in_sem, win_sem, wout_sem, agx_s, agx_r, agp_s, agp_r, agr_s, agr_r,
+               ps_s, ps_r, ns_s, ns_r, fs_s, fs_r, ds_s, ds_r):
     me = lax.axis_index('grp')
     partner = me + 1 - 2 * (me % 2)
     cross = (me + 2) % 4
+    diag = (partner + 2) % 4
 
     def win_copy(i, width):
         src = win_hbm.at[:, pl.ds(i * F_CHUNK, width)]
@@ -268,14 +270,18 @@
     m_copy.start()
     tail = FFN_LOC - (N_F - 1) * F_CHUNK
     widths = [F_CHUNK] * (N_F - 1) + [tail]
-    for i in range(RING):
+    first_copies = [pltpu.make_async_copy(win_hbm.at[part, pl.ds(0, F_CHUNK)], win_buf.at[0, part],
+                                          win_sem.at[part * RING]) for part in range(2)]
+    for cp in first_copies:
+        cp.start(priority=1)
+    for i in range(1, RING):
         win_copy(i, widths[i]).start(priority=1)
     h_copy.start()
 
     barrier = pltpu.get_barrier_semaphore()
-    for peer in (partner, cross):
+    for peer in (partner, cross, diag):
         pl.semaphore_signal(barrier, inc=1, device_id={'grp': peer}, device_id_type=pl.DeviceIdType.MESH)
-    pl.semaphore_wait(barrier, 2)
+    pl.semaphore_wait(barrier, 3)
 
     def send(src, dst, ssem, rsem, peer):
         return pltpu.make_async_remote_copy(src_ref=src, dst_ref=dst, send_sem=ssem, recv_sem=rsem,
@@ -342,8 +348,11 @@
     for i in range(N_T):
         if i == 1:
             pair_copy.wait()
-        win_copy(i, widths[i]).wait()
+        if i > 0:
+            win_copy(i, widths[i]).wait()
         for part in range(2):
+            if i == 0:
+                first_copies[part].wait()
             wint_buf[i, part] = win_buf[i % RING, part].T
         if i + RING < N_F:
             win_copy(i + RING, widths[i + RING]).start(priority=1)
@@ -375,31 +384,44 @@
         wout_copy(j).wait()
     h_copy.wait()
 
-    def piece(k):
-        return pl.ds(D_EDGES[k], D_EDGES[k + 1] - D_EDGES[k])
-
-    def block_send(src, dst, ssem, rsem, peer):
-        return [send(src.at[:, piece(k)], dst.at[:, piece(k)], ssem.at[k], rsem.at[k], peer) for k in range(N_D)]
+    def piece(k, shared=False):
+        start = max(D_EDGES[k], DIRECT) if shared else D_EDGES[k]
+        return pl.ds(start, D_EDGES[k + 1] - start)
+
+    def block_send(src, dst, ssem, rsem, peer, shared=True):
+        return [send(src.at[:, piece(k, shared)], dst.at[:, piece(k, shared)], ssem.at[k], rsem.at[k], peer) for k in range(N_D)]
 
     pair_copies = block_send(pair_send, pair_recv, ps_s, ps_r, partner)
-    near_copies = block_send(near_send, near_recv, ns_s, ns_r, partner)
+    near_copies = block_send(near_send, near_recv, ns_s, ns_r, partner, shared=False)
     far_copies = block_send(far_send, far_recv, fs_s, fs_r, cross)
 
+    direct_copies = [send(direct_send.at[pl.ds(n * ROWS, ROWS)], direct_recv.at[pl.ds(n * ROWS, ROWS)],
+                          ds_s.at[n], ds_r.at[n], (cross, diag)[n]) for n in range(2)]
+
+    def down(rows, k):
+        return jnp.dot(g_buf[rows, :], wout_buf[:, piece(k)], preferred_element_type=F32)
+
     def remote_block(k):
-        part = jnp.dot(g_buf[2 * ROWS:, :], wout_buf[:, piece(k)], preferred_element_type=F32)
-        far_keep[:, piece(k)] = part[:ROWS]
-        pair_send[:, piece(k)] = part[ROWS:].astype(BF16)
+        part = down(slice(2 * ROWS, 4 * ROWS), k)
+        if k == 0:
+            direct_send[...] = part[:, :DIRECT].astype(BF16)
+            for cp in direct_copies:
+                cp.start()
+            part = part[:, DIRECT:]
+        far_keep[:, piece(k, True)] = part[:ROWS]
+        pair_send[:, piece(k, True)] = part[ROWS:].astype(BF16)
         pair_copies[k].start()
 
     def local_block(k):
-        part = jnp.dot(g_buf[:2 * ROWS, :], wout_buf[:, piece(k)], preferred_element_type=F32)
+        part = down(slice(0, 2 * ROWS), k)
         own_acc[:, piece(k)] = part[:ROWS] + h_ref[:, piece(k)]
         near_send[:, piece(k)] = part[ROWS:].astype(BF16)
         near_copies[k].start()
 
     def pair_sum(k):
+        cols = piece(k, True)
         pair_copies[k].wait_recv()
-        far_send[:, piece(k)] = (far_keep[:, piece(k)] + pair_recv[:, piece(k)].astype(F32)).astype(BF16)
+        far_send[:, cols] = (far_keep[:, cols] + pair_recv[:, cols].astype(F32)).astype(BF16)
         far_copies[k].start()
 
     steps = [(remote_block, k) for k in range(N_D)] + [(local_block, k) for k in range(N_D)]
@@ -407,11 +429,17 @@
         step(k)
         if 0 <= n - PAIR_LAG < N_D:
             pair_sum(n - PAIR_LAG)
+    for cp in direct_copies:
+        cp.wait()
     for k in range(N_D):
         near_copies[k].wait_recv()
+        near = own_acc[:, piece(k)] + near_recv[:, piece(k)].astype(F32)
+        if k == 0:
+            direct = direct_recv[...].astype(F32)
+            y_ref[:, :DIRECT] = (near[:, :DIRECT] + direct[:ROWS] + direct[ROWS:]).astype(BF16)
+            near = near[:, DIRECT:]
         far_copies[k].wait_recv()
-        y_ref[:, piece(k)] = (own_acc[:, piece(k)] + near_recv[:, piece(k)].astype(F32)
-                              + far_recv[:, piece(k)].astype(F32)).astype(BF16)
+        y_ref[:, piece(k, True)] = (near + far_recv[:, piece(k, True)].astype(F32)).astype(BF16)
     for k in range(N_D):
         pair_copies[k].wait_send()
         near_copies[k].wait_send()
@@ -441,9 +469,10 @@
             pltpu.VMEM(piece, BF16), pltpu.VMEM(piece, BF16),
             pltpu.VMEM(piece, F32), pltpu.VMEM(piece, BF16), pltpu.VMEM(piece, BF16),
             pltpu.VMEM(piece, F32),
-            dma((2,)), dma((RING,)), dma((N_W,)),
+            pltpu.VMEM((2 * ROWS, DIRECT), BF16), pltpu.VMEM((2 * ROWS, DIRECT), BF16),
+            dma((2,)), dma((RING + 1,)), dma((N_W,)),
             dma((AG_PIECES,)), dma((AG_PIECES,)), dma, dma, dma((AG_PIECES,)), dma((AG_PIECES,)),
-            dma((N_D,)), dma((N_D,)), dma((N_D,)), dma((N_D,)), dma((N_D,)), dma((N_D,)),
+            dma((N_D,)), dma((N_D,)), dma((N_D,)), dma((N_D,)), dma((N_D,)), dma((N_D,)), dma((2,)), dma((2,)),
         ],
         compiler_params=pltpu.CompilerParams(vmem_limit_bytes=50 * 1024 * 1024, collective_id=0, has_side_effects=True),
         name="mlp_block",

time: 43.5 us -> 43.2 us (level)
  no operation moved by 1% of the time
where the time goes in v5:
time: 43.2 us; the launch traced here: 43 us
  Pallas kernels  41.7 us (97%)
  local copies, waits for them, and re-layouts  0.71 us (2%)
  between operations  0.65 us (2%)
    pallas_call x1, Pallas kernels, mlp(): pl.pallas_call(mlp_kernel, out_shape=jax.ShapeDtypeStruct((ROWS, HIDDEN),...  24.4 us
    pallas_call x1, Pallas kernels, attention(): pl.pallas_call(attn_kernel, out_shape=(jax.ShapeDtypeStruct((HBM_ROWS, HI...  17.3 us

profile of v5, /device:TPU:0, one launch (start us, length us, event | category | flops | bytes accessed | tf_op | source)
XLA Modules:
  0.0 43.0 jit_solution(11806911310515012049)
XLA Ops:
  0.6 17.3 %attn_block.1 = (f32[2048,2048]{1,0:T(8,128)}, bf16[2048,2048]{1,0:T(8,128)(2,1)}, bf16[64,512,128]{2,1,0:T(8,128)(2,1)}, bf16[64,512,128]{2,1,0:T(8,128)(2,1)}) custom-call(s32[64]{0:T(128)} %len_ref.1, f32[1,128]{1,0:T(1,128)} %constant.2.clone.freq_hbm, bf16[64,2048]{1,0:T(8,128)(2,1)} %x_hbm.1, bf16[2048]{0:T(1024)(128)(2,1)} %ga_hbm.1, ...), custom_call_target="tpu_custom_call" | custom-call | tf_op jit(solution)/shard_map/attn_block/pallas_call | solution.py:225
  18.0 24.4 %mlp_block.1 = bf16[64,2048]{1,0:T(8,128)(2,1)S(1)} custom-call(bf16[2048,2048]{1,0:T(8,128)(2,1)} %get-tuple-element.7.m_hbm, f32[2048,2048]{1,0:T(8,128)} %get-tuple-element.8.h_hbm, bf16[2,2752,2048]{2,1,0:T(8,128)(2,1)} %win_hbm.1, bf16[2752,2048]{1,0:T(8,128)(2,1)} %wout_hbm.1), custom_call_target="tpu_custom_call" | custom-call | tf_op jit(solution)/shard_map/mlp_block/pallas_call | solution.py:454
  42.3 0.7 %copy.16 = bf16[64,2048]{1,0:T(8,128)(2,1)} copy(bf16[64,2048]{1,0:T(8,128)(2,1)S(1)} %mlp_block.1) | data formatting | bytes 524288

commit v6 on v5

--- a/solution.py
+++ b/solution.py
@@ -34,11 +34,11 @@
 AG_COLS = HIDDEN // AG_PIECES
 K_PARTS = ((0, HIDDEN // 2), (HIDDEN // 2, HIDDEN // 2))
 RING = 4
-CUT = 6
+CUT = 4
 N_T = 9
 N_W = 4
 W_ROWS = FFN_LOC // N_W
-RELAY_AT = (5, 7)
+RELAY_AT = (4, 6)
 HBM_ROWS = 2048
 F32 = jnp.float32
 BF16 = jnp.bfloat16

time: 43.2 us -> 42.8 us (level)
  no operation moved by 1% of the time
where the time goes in v6:
time: 42.8 us; the launch traced here: 42.7 us
  Pallas kernels  41.3 us (96%)
  local copies, waits for them, and re-layouts  0.71 us (2%)
  between operations  0.65 us (2%)
    pallas_call x1, Pallas kernels, mlp(): pl.pallas_call(mlp_kernel, out_shape=jax.ShapeDtypeStruct((ROWS, HIDDEN),...  24 us
    pallas_call x1, Pallas kernels, attention(): pl.pallas_call(attn_kernel, out_shape=(jax.ShapeDtypeStruct((HBM_ROWS, HI...  17.3 us

profile of v6, /device:TPU:0, one launch (start us, length us, event | category | flops | bytes accessed | tf_op | source)
XLA Modules:
  0.0 42.7 jit_solution(1432686459717699333)
XLA Ops:
  0.6 17.3 %attn_block.1 = (f32[2048,2048]{1,0:T(8,128)}, bf16[2048,2048]{1,0:T(8,128)(2,1)}, bf16[64,512,128]{2,1,0:T(8,128)(2,1)}, bf16[64,512,128]{2,1,0:T(8,128)(2,1)}) custom-call(s32[64]{0:T(128)} %len_ref.1, f32[1,128]{1,0:T(1,128)} %constant.2.clone.freq_hbm, bf16[64,2048]{1,0:T(8,128)(2,1)} %x_hbm.1, bf16[2048]{0:T(1024)(128)(2,1)} %ga_hbm.1, ...), custom_call_target="tpu_custom_call" | custom-call | tf_op jit(solution)/shard_map/attn_block/pallas_call | solution.py:225
  18.0 24.0 %mlp_block.1 = bf16[64,2048]{1,0:T(8,128)(2,1)S(1)} custom-call(bf16[2048,2048]{1,0:T(8,128)(2,1)} %get-tuple-element.7.m_hbm, f32[2048,2048]{1,0:T(8,128)} %get-tuple-element.8.h_hbm, bf16[2,2752,2048]{2,1,0:T(8,128)(2,1)} %win_hbm.1, bf16[2752,2048]{1,0:T(8,128)(2,1)} %wout_hbm.1), custom_call_target="tpu_custom_call" | custom-call | tf_op jit(solution)/shard_map/mlp_block/pallas_call | solution.py:454
  42.0 0.7 %copy.16 = bf16[64,2048]{1,0:T(8,128)(2,1)} copy(bf16[64,2048]{1,0:T(8,128)(2,1)S(1)} %mlp_block.1) | data formatting | bytes 524288

commit v7 on v6

--- a/solution.py
+++ b/solution.py
@@ -183,16 +183,17 @@
         v_copy(i).wait()
         fetch(N_QKV + i + WINDOW)
         if i >= OUT_LAG:
-            ko_copy(i - OUT_LAG).start()
-            vo_copy(i - OUT_LAG).start()
+            ready = [i - OUT_LAG] if i < N_SEQ - 1 else range(i - OUT_LAG, N_SEQ - 1)
+            for j in ready:
+                ko_copy(j).start()
+                vo_copy(j).start()
         insert(i)
         raw = scores(i)
         if i > 0:
             weighted_values(i - 1, probs)
         probs = probabilities(i, raw)
-    for i in range(N_SEQ - OUT_LAG, N_SEQ):
-        ko_copy(i).start()
-        vo_copy(i).start()
+    ko_copy(N_SEQ - 1).start()
+    vo_copy(N_SEQ - 1).start()
     weighted_values(N_SEQ - 1, probs)
 
     for h in range(HEADS):
@@ -365,10 +366,10 @@
     for j in range(N_T + RING - N_F, N_W):
         wout_copy(j).start(priority=1)
     local_ffn(N_T - 1)
+    if len(RELAY_AT) < 3:
+        relay(2)
     for i in range(N_T, N_F):
         win_copy(i, widths[i]).wait()
-    if len(RELAY_AT) < 3:
-        relay(2)
     for p in range(2):
         relays[p].wait_recv()
     remote_phase(0, 0, CUT)

time: 42.8 us -> 42.8 us (level)
  no operation moved by 1% of the time
where the time goes in v7:
time: 42.8 us; the launch traced here: 42.7 us
  Pallas kernels  41.3 us (96%)
  local copies, waits for them, and re-layouts  0.71 us (2%)
  between operations  0.65 us (2%)
    pallas_call x1, Pallas kernels, mlp(): pl.pallas_call(mlp_kernel, out_shape=jax.ShapeDtypeStruct((ROWS, HIDDEN),...  24 us
    pallas_call x1, Pallas kernels, attention(): pl.pallas_call(attn_kernel, out_shape=(jax.ShapeDtypeStruct((HBM_ROWS, HI...  17.3 us

profile of v7, /device:TPU:0, one launch (start us, length us, event | category | flops | bytes accessed | tf_op | source)
XLA Modules:
  0.0 42.7 jit_solution(9034160713162764959)
XLA Ops:
  0.6 17.3 %attn_block.1 = (f32[2048,2048]{1,0:T(8,128)}, bf16[2048,2048]{1,0:T(8,128)(2,1)}, bf16[64,512,128]{2,1,0:T(8,128)(2,1)}, bf16[64,512,128]{2,1,0:T(8,128)(2,1)}) custom-call(s32[64]{0:T(128)} %len_ref.1, f32[1,128]{1,0:T(1,128)} %constant.2.clone.freq_hbm, bf16[64,2048]{1,0:T(8,128)(2,1)} %x_hbm.1, bf16[2048]{0:T(1024)(128)(2,1)} %ga_hbm.1, ...), custom_call_target="tpu_custom_call" | custom-call | tf_op jit(solution)/shard_map/attn_block/pallas_call | solution.py:226
  18.0 24.0 %mlp_block.1 = bf16[64,2048]{1,0:T(8,128)(2,1)S(1)} custom-call(bf16[2048,2048]{1,0:T(8,128)(2,1)} %get-tuple-element.7.m_hbm, f32[2048,2048]{1,0:T(8,128)} %get-tuple-element.8.h_hbm, bf16[2,2752,2048]{2,1,0:T(8,128)(2,1)} %win_hbm.1, bf16[2752,2048]{1,0:T(8,128)(2,1)} %wout_hbm.1), custom_call_target="tpu_custom_call" | custom-call | tf_op jit(solution)/shard_map/mlp_block/pallas_call | solution.py:455
  42.0 0.7 %copy.16 = bf16[64,2048]{1,0:T(8,128)(2,1)} copy(bf16[64,2048]{1,0:T(8,128)(2,1)S(1)} %mlp_block.1) | data formatting | bytes 524288
